TPU v7x, 512 devices: a 8x2x16 block of a 8x8x16 slice. The times are simulated.
512 devices in a mesh: grp: 2 (over y), gx: 16 (over z), gy: 8 (over x), gz: 2 (over core).
Axes of the slice: x: 8, y: 2, z: 16, core: 2. Of those that a mesh axis runs over, the one named last changes fastest.
The devices are a block of a 8x8x16 slice.
Arguments:
- design: int32 [64, 64, 256], P(('grp', 'gx'), 'gy', 'gz'), parts along dimension 0, may hold values from 0 to 15
- supports: int32 [64, 64, 256], P(('grp', 'gx'), 'gy', 'gz'), parts along dimension 0, may hold values 0 or 1
- body_load: float32 [12, 3, 32, 64, 256], P('grp', None, 'gx', 'gy', 'gz'), parts along dimension 0, may hold values from -6 to 6
- start: float32 [12, 3, 32, 64, 256], P('grp', None, 'gx', 'gy', 'gz'), parts along dimension 0, may hold values from -1.8 to 1.8
- load_nodes: int32 [12, 16], P('grp'), parts along dimension 0, may hold values from 0 to 524287
- load_values: float32 [12, 16, 3], P('grp'), parts along dimension 0, may hold values from -24 to 24
Outputs:
- solution: float32 [12, 3, 32, 64, 256], P('grp', None, 'gx', 'gy', 'gz'), parts along dimension 0
- residual: float32 [12, 3, 32, 64, 256], P('grp', None, 'gx', 'gy', 'gz'), parts along dimension 0
There are 2 independent parts, one for each index of `grp`. A program takes and returns all parts, laid end to end along the dimension named above; each array names one. Nothing has to cross between parts.
Inputs may be any that keep to these rules, and one draw needn't show every extreme that they name: `supports`: 1 where all three displacements of the node are held fixed. `load_nodes`: flat index (i * 64 + j) * 256 + k of a loaded node; a node may be named several times.
All inputs are finite; a program needn't handle non-finite values. No bound on the sum of `supports` on one device may be relied on, other than what follows from the above.
Results may differ from a plain program's by a relative error of at most 0.0003.
Values sent between devices are 32-bit elements; how exact they have to be, the bound alone decides.
A program may use at most 64 MiB of HBM per device.

v0:
```python
import jax
import jax.numpy as jnp
import numpy as np
from jax import lax
from jax.sharding import PartitionSpec as P

LEVELS = 16
ITERS = 2


soft_modulus = 0.05
poisson_ratio = 0.3
highest = lax.Precision.HIGHEST


def padded_2(block, sides, width):
    for axis, dim in sides:
        count = lax.axis_size(axis)
        forward = [(i, i + 1) for i in range(count - 1)]
        backward = [(target, source) for source, target in forward]
        low = lax.ppermute(
            lax.slice_in_dim(block, block.shape[dim] - width, None, axis=dim), axis, forward
        )
        high = lax.ppermute(lax.slice_in_dim(block, 0, width, axis=dim), axis, backward)
        block = jnp.concatenate([low, block, high], axis=dim)
    return block


def one_axis_at_a_time(shard, axes):
    for axis in axes:
        shard = lax.psum(shard, axis)
    return shard


def corner_list():
    return [(first, second, third) for first in (0, 1) for second in (0, 1) for third in (0, 1)]


def element_matrix():
    lame_first = poisson_ratio / ((1.0 + poisson_ratio) * (1.0 - 2.0 * poisson_ratio))
    shear_modulus = 1.0 / (2.0 * (1.0 + poisson_ratio))
    elastic = np.zeros((6, 6))
    elastic[:3, :3] = lame_first
    for axis_dim in range(3):
        elastic[axis_dim, axis_dim] += 2.0 * shear_modulus
        elastic[3 + axis_dim, 3 + axis_dim] = shear_modulus
    gauss_points = [0.5 - 0.5 / np.sqrt(3.0), 0.5 + 0.5 / np.sqrt(3.0)]
    corners = corner_list()
    matrix_total = np.zeros((24, 24))
    for first_point in gauss_points:
        for second_point in gauss_points:
            for third_point in gauss_points:
                points = (first_point, second_point, third_point)
                strain = np.zeros((6, 24))
                for number, corner in enumerate(corners):
                    values = [
                        points[axis_dim] if corner[axis_dim] else 1.0 - points[axis_dim]
                        for axis_dim in range(3)
                    ]
                    slopes = [1.0 if corner[axis_dim] else -1.0 for axis_dim in range(3)]
                    grad_first = slopes[0] * values[1] * values[2]
                    grad_second = values[0] * slopes[1] * values[2]
                    grad_third = values[0] * values[1] * slopes[2]
                    column = 3 * number
                    strain[0, column] = grad_first
                    strain[1, column + 1] = grad_second
                    strain[2, column + 2] = grad_third
                    strain[3, column] = grad_second
                    strain[3, column + 1] = grad_first
                    strain[4, column + 1] = grad_third
                    strain[4, column + 2] = grad_second
                    strain[5, column] = grad_third
                    strain[5, column + 2] = grad_first
                matrix_total = matrix_total + strain.T @ elastic @ strain / 8.0
    return jnp.asarray(matrix_total, dtype=jnp.float32)


def stiffness_of(design):
    density = (design.astype(jnp.float32) + 1.0) / LEVELS
    return soft_modulus + (1.0 - soft_modulus) * density * density * density


def crop(array, width):
    return array[
        ...,
        width : array.shape[-3] - width,
        width : array.shape[-2] - width,
        width : array.shape[-1] - width,
    ]


def bordered(array, width):
    return padded_2(array, (("gx", 2), ("gy", 3), ("gz", 4)), width)


def with_statics(fields, stiffness, movable, width):
    statics = jnp.stack([stiffness, movable])[None]
    members = fields.shape[0] * 3
    joined = jnp.concatenate([fields.reshape((1, members) + fields.shape[2:]), statics], axis=1)
    wide = bordered(joined, width)
    fields_wide = wide[0, :members].reshape((fields.shape[0], 3) + wide.shape[2:])
    return (fields_wide, wide[0, members], wide[0, members + 1])


def stiff_apply(padded, moduli, element_stiffness):
    span_first, span_second, span_third = padded.shape[-3:]
    corners = corner_list()
    results = []
    for member in range(padded.shape[0]):
        single = padded[member]
        stacked = jnp.concatenate(
            [
                single[
                    :,
                    corner[0] : span_first - 1 + corner[0],
                    corner[1] : span_second - 1 + corner[1],
                    corner[2] : span_third - 1 + corner[2],
                ]
                for corner in corners
            ],
            axis=0,
        )
        forces = jnp.einsum("ij,jxyz->ixyz", element_stiffness, stacked, precision=highest)
        forces = forces * moduli[None, : span_first - 1, : span_second - 1, : span_third - 1]
        accumulated = jnp.zeros((3, span_first - 2, span_second - 2, span_third - 2), jnp.float32)
        for number, corner in enumerate(corners):
            accumulated = (
                accumulated
                + forces[
                    3 * number : 3 * number + 3,
                    1 - corner[0] : span_first - 1 - corner[0],
                    1 - corner[1] : span_second - 1 - corner[1],
                    1 - corner[2] : span_third - 1 - corner[2],
                ]
            )
        results.append(accumulated)
    return jnp.stack(results)


def operate(padded, moduli, movable_pad, element_stiffness):
    forces = stiff_apply(padded * movable_pad, moduli, element_stiffness)
    inner = crop(movable_pad, 1)
    return inner * forces + (1.0 - inner) * crop(padded, 1)


def inverse_diagonal(moduli, movable_inner, element_stiffness):
    span_first, span_second, span_third = moduli.shape
    adjacent = jnp.zeros((span_first - 2, span_second - 2, span_third - 2), jnp.float32)
    for corner in corner_list():
        adjacent = (
            adjacent
            + moduli[
                1 - corner[0] : span_first - 1 - corner[0],
                1 - corner[1] : span_second - 1 - corner[1],
                1 - corner[2] : span_third - 1 - corner[2],
            ]
        )
    guarded = jnp.where(movable_inner > 0, adjacent, 1.0)
    return movable_inner / (element_stiffness[0, 0] * guarded) + (1.0 - movable_inner)


def gram_matrix(first, second):
    return jnp.einsum("iaxyz,jaxyz->ij", first, second, precision=highest)


def combine(fields, coeffs):
    return jnp.einsum("jaxyz,ji->iaxyz", fields, coeffs, precision=highest)


def small_solve(matrix, right):
    factor = jnp.linalg.cholesky(matrix)
    middle = lax.linalg.triangular_solve(factor, right, left_side=True, lower=True)
    return lax.linalg.triangular_solve(factor, middle, left_side=True, lower=True, transpose_a=True)


def pair_sums(direction, applied, residual):
    return (
        one_axis_at_a_time(gram_matrix(direction, applied), ("gx", "gy", "gz")),
        one_axis_at_a_time(gram_matrix(direction, residual), ("gx", "gy", "gz")),
    )


def owned_load(body_load, load_nodes, load_values):
    extents = body_load.shape[2:]
    across_second = extents[1] * lax.axis_size("gy")
    across_third = extents[2] * lax.axis_size("gz")
    first_index = lax.axis_index("gx") * extents[0] + lax.broadcasted_iota(jnp.int32, extents, 0)
    second_index = lax.axis_index("gy") * extents[1] + lax.broadcasted_iota(jnp.int32, extents, 1)
    third_index = lax.axis_index("gz") * extents[2] + lax.broadcasted_iota(jnp.int32, extents, 2)
    numbers = ((first_index * across_second + second_index) * across_third + third_index).reshape(
        -1
    )
    matches = (load_nodes[:, :, None] == numbers[None, None, :]).astype(jnp.float32)
    points = jnp.einsum("cla,cln->can", load_values, matches, precision=highest)
    return body_load + points.reshape(body_load.shape)


def shards(design, supports, body_load, start, load_nodes, load_values):
    element_stiffness = element_matrix()
    stiffness = stiffness_of(design)
    movable = 1.0 - supports.astype(jnp.float32)
    loading = movable * owned_load(body_load, load_nodes, load_values)
    start_wide, moduli, movable_pad = with_statics(start, stiffness, movable, 1)
    residual = loading - operate(start_wide, moduli, movable_pad, element_stiffness)
    scaling = inverse_diagonal(moduli, movable, element_stiffness)
    direction = scaling * residual
    solution = start
    for turn_index in range(ITERS):
        final_turn = turn_index + 1 == ITERS
        applied = operate(bordered(direction, 1), moduli, movable_pad, element_stiffness)
        curvature, projection = pair_sums(direction, applied, residual)
        step_size = small_solve(curvature, projection)
        solution = solution + combine(direction, step_size)
        updated = residual - combine(applied, step_size)
        if not final_turn:
            scaled = scaling * updated
            coupling = one_axis_at_a_time(gram_matrix(applied, scaled), ("gx", "gy", "gz"))
            direction = scaled + combine(direction, -small_solve(curvature, coupling))
        residual = updated
    return (solution, residual)


def solution(mesh):
    in_specs = (
        P(("grp", "gx"), "gy", "gz"),
        P(("grp", "gx"), "gy", "gz"),
        P("grp", None, "gx", "gy", "gz"),
        P("grp", None, "gx", "gy", "gz"),
        P("grp", None),
        P("grp", None, None),
    )
    out_specs = (P("grp", None, "gx", "gy", "gz"), P("grp", None, "gx", "gy", "gz"))
    return jax.shard_map(shards, mesh=mesh, in_specs=in_specs, out_specs=out_specs, check_vma=False)
```

profile of v0, /device:TPU:65, one launch (start us, length us, event | category | flops | bytes accessed | tf_op | source)
XLA Modules:
  0.0 326.6 jit_solution(13636758643104474152)
XLA Ops:
  3.0 1.3 collective-permute-start.1
  4.3 7.2 %collective-permute-start = (f32[1,20,1,8,128]{4,3,2,1,0:T(8,128)S(1)}, f32[1,20,1,8,128]{4,3,2,1,0:T(8,128)S(1)}, u32[]{:S(2)}, u32[]{:S(2)}) collective-permute-start(f32[1,20,1,8,128]{4,3,2,1,0:T(8,128)S(1)} %get-tuple-element.67), channel_id=1, source_target_pairs={{0,16},{16,32},{32,48},{48,64},{64,80},{80,96},{96,112},{112,128},... | collective-permute-start | bytes 245768 | tf_op jit(solution)/shard_map/ppermute | solution.py:21
  11.6 1.4 collective-permute-done
  14.0 1.3 collective-permute-start.3
  15.4 4.0 %collective-permute-start.2 = (f32[1,20,4,1,128]{4,3,2,1,0:T(1,128)S(1)}, f32[1,20,4,1,128]{4,3,2,1,0:T(1,128)S(1)}, u32[]{:S(2)}, u32[]{:S(2)}) collective-permute-start(f32[1,20,4,1,128]{4,3,2,1,0:T(1,128)S(1)} %get-tuple-element.61), channel_id=1, source_target_pairs={{0,2},{2,4},{4,6},{6,8},{8,10},{10,12},{12,14},{1,3},{3,5},{5,7},{... | collective-permute-start | bytes 122888 | tf_op jit(solution)/shard_map/ppermute | solution.py:21
  22.2 42.5 %collective-permute-start.5 = (f32[1,20,4,10,1]{1,2,4,3,0:T(4,128)S(1)}, f32[1,20,4,10,1]{1,2,4,3,0:T(4,128)S(1)}, u32[]{:S(2)}, u32[]{:S(2)}) collective-permute-start(f32[1,20,4,10,1]{1,2,4,3,0:T(4,128)S(1)} %copy.259), channel_id=1, source_target_pairs={{1,0},{3,2},{5,4},{7,6},{9,8},{11,10},{13,12},{15,14},{17,16},{19,... | collective-permute-start | bytes 9608 | tf_op jit(solution)/shard_map/ppermute | solution.py:24
  65.0 1.4 collective-permute-start.4
  73.7 1.1 fusion.44
  77.0 1.1 fusion.50
  79.1 1.1 fusion.46
  80.2 1.1 fusion.54
  81.2 1.9 fusion.12
  84.2 1.3 collective-permute-start.7
  85.5 4.7 %collective-permute-start.6 = (f32[6,3,1,8,128]{4,3,2,1,0:T(8,128)S(1)}, f32[6,3,1,8,128]{4,3,2,1,0:T(8,128)S(1)}, u32[]{:S(2)}, u32[]{:S(2)}) collective-permute-start(f32[6,3,1,8,128]{4,3,2,1,0:T(8,128)S(1)} %get-tuple-element.71), channel_id=1, source_target_pairs={{0,16},{16,32},{32,48},{48,64},{64,80},{80,96},{96,112},{112,128},... | collective-permute-start | bytes 221192 | tf_op jit(solution)/shard_map/ppermute | solution.py:21
  90.2 1.4 collective-permute-done.6
  91.6 1.3 collective-permute-start.9
  93.0 4.6 %collective-permute-start.8 = (f32[6,3,4,1,128]{4,3,2,1,0:T(1,128)S(1)}, f32[6,3,4,1,128]{4,3,2,1,0:T(1,128)S(1)}, u32[]{:S(2)}, u32[]{:S(2)}) collective-permute-start(f32[6,3,4,1,128]{4,3,2,1,0:T(1,128)S(1)} %get-tuple-element.65), channel_id=1, source_target_pairs={{0,2},{2,4},{4,6},{6,8},{8,10},{10,12},{12,14},{1,3},{3,5},{5,7},{... | collective-permute-start | bytes 110600 | tf_op jit(solution)/shard_map/ppermute | solution.py:21
  99.5 4.3 %collective-permute-start.11 = (f32[6,3,4,10,1]{3,2,4,1,0:T(4,128)S(1)}, f32[6,3,4,10,1]{3,2,4,1,0:T(4,128)S(1)}, u32[]{:S(2)}, u32[]{:S(2)}) collective-permute-start(f32[6,3,4,10,1]{3,2,4,1,0:T(4,128)S(1)} %copy.281), channel_id=1, source_target_pairs={{1,0},{3,2},{5,4},{7,6},{9,8},{11,10},{13,12},{15,14},{17,16},{19,... | collective-permute-start | bytes 8648 | tf_op jit(solution)/shard_map/ppermute | solution.py:24
  104.4 1.3 collective-permute-start.10
  109.6 1.1 fusion.32
  111.2 1.1 fusion.42
  112.8 1.1 fusion.40
  114.3 1.1 fusion.38
  115.9 1.1 fusion.36
  118.6 1.5 fusion.6
  120.7 12.6 %multiply_add_fusion.1 = f32[6,3,2,8,128]{4,3,2,1,0:T(8,128)S(1)} fusion(f32[6,3,2,8,128]{4,3,2,1,0:T(8,128)S(1)} %get-tuple-element.31, f32[6,3,2,8,128]{4,3,2,1,0:T(8,128)S(1)} %constant_dynamic-update-slice_fusion.102, f32[2,8,128]{2,1,0:T(8,128)S(1)} %get-tuple-element.74, f32[2,8,128]{2,1,0:T(8,128)S(1)} %get-tuple-element.73), kind=kLoop, calls=%fused_computation.301 | loop fusion | flops 110592 | bytes 458752 | tf_op jit(solution)/shard_map/add | solution.py:143
  133.9 22.8 %all-reduce.1 = (f32[6,6]{1,0:T(8,128)S(1)}, f32[6,6]{0,1:T(8,128)S(1)}) all-reduce(f32[6,6]{1,0:T(8,128)S(1)} %convolution_bitcast_fusion.6, f32[6,6]{0,1:T(8,128)S(1)} %convolution_bitcast_fusion.7), channel_id=1, replica_groups=mesh['grp'=2,'gx'=16,'gy'=8,'gz'=2] {'gx'}, use_global_device_ids=true, to_apply=%region_5.0 | all-reduce | flops 72 | bytes 576 | tf_op jit(solution)/shard_map/psum | solution.py:31
  156.7 16.3 %all-reduce.3 = (f32[6,6]{1,0:T(8,128)S(1)}, f32[6,6]{0,1:T(8,128)S(1)}) all-reduce(f32[6,6]{1,0:T(8,128)S(1)} %get-tuple-element.19, f32[6,6]{0,1:T(8,128)S(1)} %get-tuple-element.20), channel_id=1, replica_groups=mesh['grp'=2,'gx'=16,'gy'=8,'gz'=2] {'gy'}, use_global_device_ids=true, to_apply=%region_6.8 | all-reduce | flops 72 | bytes 576 | tf_op jit(solution)/shard_map/psum | solution.py:31
  173.0 13.7 %all-reduce.5 = (f32[6,6]{1,0:T(8,128)S(1)}, f32[6,6]{0,1:T(8,128)S(1)}) all-reduce(f32[6,6]{1,0:T(8,128)S(1)} %get-tuple-element.23, f32[6,6]{0,1:T(8,128)S(1)} %get-tuple-element.24), channel_id=1, replica_groups=mesh['grp'=2,'gx'=16,'gy'=8,'gz'=2] {'gz'}, use_global_device_ids=true, to_apply=%region_7.9 | all-reduce | flops 72 | bytes 576 | tf_op jit(solution)/shard_map/psum | solution.py:31
  190.5 20.2 %psum.111 = f32[6,6]{1,0:T(8,128)S(1)} all-reduce(f32[6,6]{1,0:T(8,128)S(1)} %convolution_bitcast_fusion.5), channel_id=1, replica_groups=mesh['grp'=2,'gx'=16,'gy'=8,'gz'=2] {'gx'}, use_global_device_ids=true, to_apply=%region_8.12 | all-reduce | flops 36 | bytes 288 | tf_op jit(solution)/shard_map/psum | solution.py:31
  210.7 11.5 %psum.112 = f32[6,6]{1,0:T(8,128)S(1)} all-reduce(f32[6,6]{1,0:T(8,128)S(1)} %psum.111), channel_id=1, replica_groups=mesh['grp'=2,'gx'=16,'gy'=8,'gz'=2] {'gy'}, use_global_device_ids=true, to_apply=%region_9.13 | all-reduce | flops 36 | bytes 288 | tf_op jit(solution)/shard_map/psum | solution.py:31
  222.1 13.1 %psum.113 = f32[6,6]{1,0:T(8,128)S(1)} all-reduce(f32[6,6]{1,0:T(8,128)S(1)} %psum.112), channel_id=1, replica_groups=mesh['grp'=2,'gx'=16,'gy'=8,'gz'=2] {'gz'}, use_global_device_ids=true, to_apply=%region_10.14 | all-reduce | flops 36 | bytes 288 | tf_op jit(solution)/shard_map/psum | solution.py:31
  236.0 1.3 collective-permute-start.13
  237.3 4.3 %collective-permute-start.12 = (f32[6,3,1,8,128]{4,3,2,1,0:T(8,128)S(1)}, f32[6,3,1,8,128]{4,3,2,1,0:T(8,128)S(1)}, u32[]{:S(2)}, u32[]{:S(2)}) collective-permute-start(f32[6,3,1,8,128]{4,3,2,1,0:T(8,128)S(1)} %get-tuple-element.69), channel_id=1, source_target_pairs={{0,16},{16,32},{32,48},{48,64},{64,80},{80,96},{96,112},{112,128},... | collective-permute-start | bytes 221192 | tf_op jit(solution)/shard_map/ppermute | solution.py:21
  241.9 1.1 collective-permute-done.12
  243.0 1.3 collective-permute-start.15
  244.3 4.0 %collective-permute-start.14 = (f32[6,3,4,1,128]{4,3,2,1,0:T(1,128)S(1)}, f32[6,3,4,1,128]{4,3,2,1,0:T(1,128)S(1)}, u32[]{:S(2)}, u32[]{:S(2)}) collective-permute-start(f32[6,3,4,1,128]{4,3,2,1,0:T(1,128)S(1)} %get-tuple-element.63), channel_id=1, source_target_pairs={{0,2},{2,4},{4,6},{6,8},{8,10},{10,12},{12,14},{1,3},{3,5},{5,7},{... | collective-permute-start | bytes 110600 | tf_op jit(solution)/shard_map/ppermute | solution.py:21
  250.3 4.3 %collective-permute-start.17 = (f32[6,3,4,10,1]{3,2,4,1,0:T(4,128)S(1)}, f32[6,3,4,10,1]{3,2,4,1,0:T(4,128)S(1)}, u32[]{:S(2)}, u32[]{:S(2)}) collective-permute-start(f32[6,3,4,10,1]{3,2,4,1,0:T(4,128)S(1)} %copy.318), channel_id=1, source_target_pairs={{1,0},{3,2},{5,4},{7,6},{9,8},{11,10},{13,12},{15,14},{17,16},{19,... | collective-permute-start | bytes 8648 | tf_op jit(solution)/shard_map/ppermute | solution.py:24
  255.1 1.3 collective-permute-start.16
  260.3 1.1 fusion.20
  261.9 1.1 fusion.30
  263.5 1.1 fusion.28
  266.7 1.1 fusion.24
  268.3 1.1 fusion.22
  269.3 1.5 fusion
  272.1 22.8 %all-reduce = (f32[6,6]{1,0:T(8,128)S(1)}, f32[6,6]{0,1:T(8,128)S(1)}) all-reduce(f32[6,6]{1,0:T(8,128)S(1)} %convolution_bitcast_fusion.3, f32[6,6]{0,1:T(8,128)S(1)} %convolution_bitcast_fusion.4), channel_id=1, replica_groups=mesh['grp'=2,'gx'=16,'gy'=8,'gz'=2] {'gx'}, use_global_device_ids=true, to_apply=%region_14.18 | all-reduce | flops 72 | bytes 576 | tf_op jit(solution)/shard_map/psum | solution.py:31
  294.9 13.0 %all-reduce.2 = (f32[6,6]{1,0:T(8,128)S(1)}, f32[6,6]{0,1:T(8,128)S(1)}) all-reduce(f32[6,6]{1,0:T(8,128)S(1)} %get-tuple-element.17, f32[6,6]{0,1:T(8,128)S(1)} %get-tuple-element.18), channel_id=1, replica_groups=mesh['grp'=2,'gx'=16,'gy'=8,'gz'=2] {'gy'}, use_global_device_ids=true, to_apply=%region_15.19 | all-reduce | flops 72 | bytes 576 | tf_op jit(solution)/shard_map/psum | solution.py:31
  307.9 13.6 %all-reduce.4 = (f32[6,6]{1,0:T(8,128)S(1)}, f32[6,6]{0,1:T(8,128)S(1)}) all-reduce(f32[6,6]{1,0:T(8,128)S(1)} %get-tuple-element.21, f32[6,6]{0,1:T(8,128)S(1)} %get-tuple-element.22), channel_id=1, replica_groups=mesh['grp'=2,'gx'=16,'gy'=8,'gz'=2] {'gz'}, use_global_device_ids=true, to_apply=%region_16.20 | all-reduce | flops 72 | bytes 576 | tf_op jit(solution)/shard_map/psum | solution.py:31
  (275 shorter events, 48.7 us)
Async XLA Ops:
  0.6 65.9 %copy-start = (f32[6,16,3]{1,2,0:T(4,128)S(1)}, f32[6,16,3]{1,2,0:T(4,128)}, u32[]{:S(2)}) copy-start(f32[6,16,3]{1,2,0:T(4,128)} %param.17) | copy-start | bytes 3460
  3.0 8.6 %collective-permute-start.1 = (f32[1,20,1,8,128]{4,3,2,1,0:T(8,128)S(1)}, f32[1,20,1,8,128]{4,3,2,1,0:T(8,128)S(1)}, u32[]{:S(2)}, u32[]{:S(2)}) collective-permute-start(f32[1,20,1,8,128]{4,3,2,1,0:T(8,128)S(1)} %get-tuple-element.68), channel_id=1, source_target_pairs={{16,0},{32,16},{48,32},{64,48},{80,64},{96,80},{112,96},{128,112},... | collective-permute-start | bytes 245768 | tf_op jit(solution)/shard_map/ppermute | solution.py:24
  4.3 8.7 %collective-permute-start = (f32[1,20,1,8,128]{4,3,2,1,0:T(8,128)S(1)}, f32[1,20,1,8,128]{4,3,2,1,0:T(8,128)S(1)}, u32[]{:S(2)}, u32[]{:S(2)}) collective-permute-start(f32[1,20,1,8,128]{4,3,2,1,0:T(8,128)S(1)} %get-tuple-element.67), channel_id=1, source_target_pairs={{0,16},{16,32},{32,48},{48,64},{64,80},{80,96},{96,112},{112,128},... | collective-permute-start | bytes 245768 | tf_op jit(solution)/shard_map/ppermute | solution.py:21
  14.0 5.4 %collective-permute-start.3 = (f32[1,20,4,1,128]{4,3,2,1,0:T(1,128)S(1)}, f32[1,20,4,1,128]{4,3,2,1,0:T(1,128)S(1)}, u32[]{:S(2)}, u32[]{:S(2)}) collective-permute-start(f32[1,20,4,1,128]{4,3,2,1,0:T(1,128)S(1)} %get-tuple-element.62), channel_id=1, source_target_pairs={{2,0},{4,2},{6,4},{8,6},{10,8},{12,10},{14,12},{3,1},{5,3},{7,5},{... | collective-permute-start | bytes 122888 | tf_op jit(solution)/shard_map/ppermute | solution.py:24
  15.4 5.1 %collective-permute-start.2 = (f32[1,20,4,1,128]{4,3,2,1,0:T(1,128)S(1)}, f32[1,20,4,1,128]{4,3,2,1,0:T(1,128)S(1)}, u32[]{:S(2)}, u32[]{:S(2)}) collective-permute-start(f32[1,20,4,1,128]{4,3,2,1,0:T(1,128)S(1)} %get-tuple-element.61), channel_id=1, source_target_pairs={{0,2},{2,4},{4,6},{6,8},{8,10},{10,12},{12,14},{1,3},{3,5},{5,7},{... | collective-permute-start | bytes 122888 | tf_op jit(solution)/shard_map/ppermute | solution.py:21
  21.8 44.7 %copy-start.6 = (s32[6,16]{1,0:T(8,128)S(1)}, s32[6,16]{1,0:T(8,128)}, u32[]{:S(2)}) copy-start(s32[6,16]{1,0:T(8,128)} %param.16) | copy-start | bytes 1156
  22.2 44.9 %collective-permute-start.5 = (f32[1,20,4,10,1]{1,2,4,3,0:T(4,128)S(1)}, f32[1,20,4,10,1]{1,2,4,3,0:T(4,128)S(1)}, u32[]{:S(2)}, u32[]{:S(2)}) collective-permute-start(f32[1,20,4,10,1]{1,2,4,3,0:T(4,128)S(1)} %copy.259), channel_id=1, source_target_pairs={{1,0},{3,2},{5,4},{7,6},{9,8},{11,10},{13,12},{15,14},{17,16},{19,... | collective-permute-start | bytes 9608 | tf_op jit(solution)/shard_map/ppermute | solution.py:24
  65.0 4.0 %copy-start.2 = (f32[6,3,2,8,128]{4,3,2,1,0:T(8,128)S(1)}, f32[6,3,2,8,128]{4,3,2,1,0:T(8,128)}, u32[]{:S(2)}) copy-start(f32[6,3,2,8,128]{4,3,2,1,0:T(8,128)} %param.15) | copy-start | bytes 442372
  65.0 3.2 collective-permute-start.4
  70.0 0.7 copy-start.5
  73.0 0.7 copy-start.3
  83.1 0.9 copy-start.4
  84.2 6.0 %collective-permute-start.7 = (f32[6,3,1,8,128]{4,3,2,1,0:T(8,128)S(1)}, f32[6,3,1,8,128]{4,3,2,1,0:T(8,128)S(1)}, u32[]{:S(2)}, u32[]{:S(2)}) collective-permute-start(f32[6,3,1,8,128]{4,3,2,1,0:T(8,128)S(1)} %get-tuple-element.72), channel_id=1, source_target_pairs={{16,0},{32,16},{48,32},{64,48},{80,64},{96,80},{112,96},{128,112},... | collective-permute-start | bytes 221192 | tf_op jit(solution)/shard_map/ppermute | solution.py:24
  85.5 6.1 %collective-permute-start.6 = (f32[6,3,1,8,128]{4,3,2,1,0:T(8,128)S(1)}, f32[6,3,1,8,128]{4,3,2,1,0:T(8,128)S(1)}, u32[]{:S(2)}, u32[]{:S(2)}) collective-permute-start(f32[6,3,1,8,128]{4,3,2,1,0:T(8,128)S(1)} %get-tuple-element.71), channel_id=1, source_target_pairs={{0,16},{16,32},{32,48},{48,64},{64,80},{80,96},{96,112},{112,128},... | collective-permute-start | bytes 221192 | tf_op jit(solution)/shard_map/ppermute | solution.py:21
  91.6 6.0 %collective-permute-start.9 = (f32[6,3,4,1,128]{4,3,2,1,0:T(1,128)S(1)}, f32[6,3,4,1,128]{4,3,2,1,0:T(1,128)S(1)}, u32[]{:S(2)}, u32[]{:S(2)}) collective-permute-start(f32[6,3,4,1,128]{4,3,2,1,0:T(1,128)S(1)} %get-tuple-element.66), channel_id=1, source_target_pairs={{2,0},{4,2},{6,4},{8,6},{10,8},{12,10},{14,12},{3,1},{5,3},{7,5},{... | collective-permute-start | bytes 110600 | tf_op jit(solution)/shard_map/ppermute | solution.py:24
  93.0 5.7 %collective-permute-start.8 = (f32[6,3,4,1,128]{4,3,2,1,0:T(1,128)S(1)}, f32[6,3,4,1,128]{4,3,2,1,0:T(1,128)S(1)}, u32[]{:S(2)}, u32[]{:S(2)}) collective-permute-start(f32[6,3,4,1,128]{4,3,2,1,0:T(1,128)S(1)} %get-tuple-element.65), channel_id=1, source_target_pairs={{0,2},{2,4},{4,6},{6,8},{8,10},{10,12},{12,14},{1,3},{3,5},{5,7},{... | collective-permute-start | bytes 110600 | tf_op jit(solution)/shard_map/ppermute | solution.py:21
  99.5 6.7 %collective-permute-start.11 = (f32[6,3,4,10,1]{3,2,4,1,0:T(4,128)S(1)}, f32[6,3,4,10,1]{3,2,4,1,0:T(4,128)S(1)}, u32[]{:S(2)}, u32[]{:S(2)}) collective-permute-start(f32[6,3,4,10,1]{3,2,4,1,0:T(4,128)S(1)} %copy.281), channel_id=1, source_target_pairs={{1,0},{3,2},{5,4},{7,6},{9,8},{11,10},{13,12},{15,14},{17,16},{19,... | collective-permute-start | bytes 8648 | tf_op jit(solution)/shard_map/ppermute | solution.py:24
  104.4 3.1 collective-permute-start.10
  236.0 5.9 %collective-permute-start.13 = (f32[6,3,1,8,128]{4,3,2,1,0:T(8,128)S(1)}, f32[6,3,1,8,128]{4,3,2,1,0:T(8,128)S(1)}, u32[]{:S(2)}, u32[]{:S(2)}) collective-permute-start(f32[6,3,1,8,128]{4,3,2,1,0:T(8,128)S(1)} %get-tuple-element.70), channel_id=1, source_target_pairs={{16,0},{32,16},{48,32},{64,48},{80,64},{96,80},{112,96},{128,112},... | collective-permute-start | bytes 221192 | tf_op jit(solution)/shard_map/ppermute | solution.py:24
  237.3 5.7 %collective-permute-start.12 = (f32[6,3,1,8,128]{4,3,2,1,0:T(8,128)S(1)}, f32[6,3,1,8,128]{4,3,2,1,0:T(8,128)S(1)}, u32[]{:S(2)}, u32[]{:S(2)}) collective-permute-start(f32[6,3,1,8,128]{4,3,2,1,0:T(8,128)S(1)} %get-tuple-element.69), channel_id=1, source_target_pairs={{0,16},{16,32},{32,48},{48,64},{64,80},{80,96},{96,112},{112,128},... | collective-permute-start | bytes 221192 | tf_op jit(solution)/shard_map/ppermute | solution.py:21
  243.0 5.7 %collective-permute-start.15 = (f32[6,3,4,1,128]{4,3,2,1,0:T(1,128)S(1)}, f32[6,3,4,1,128]{4,3,2,1,0:T(1,128)S(1)}, u32[]{:S(2)}, u32[]{:S(2)}) collective-permute-start(f32[6,3,4,1,128]{4,3,2,1,0:T(1,128)S(1)} %get-tuple-element.64), channel_id=1, source_target_pairs={{2,0},{4,2},{6,4},{8,6},{10,8},{12,10},{14,12},{3,1},{5,3},{7,5},{... | collective-permute-start | bytes 110600 | tf_op jit(solution)/shard_map/ppermute | solution.py:24
  244.3 5.1 %collective-permute-start.14 = (f32[6,3,4,1,128]{4,3,2,1,0:T(1,128)S(1)}, f32[6,3,4,1,128]{4,3,2,1,0:T(1,128)S(1)}, u32[]{:S(2)}, u32[]{:S(2)}) collective-permute-start(f32[6,3,4,1,128]{4,3,2,1,0:T(1,128)S(1)} %get-tuple-element.63), channel_id=1, source_target_pairs={{0,2},{2,4},{4,6},{6,8},{8,10},{10,12},{12,14},{1,3},{3,5},{5,7},{... | collective-permute-start | bytes 110600 | tf_op jit(solution)/shard_map/ppermute | solution.py:21
  250.3 6.7 %collective-permute-start.17 = (f32[6,3,4,10,1]{3,2,4,1,0:T(4,128)S(1)}, f32[6,3,4,10,1]{3,2,4,1,0:T(4,128)S(1)}, u32[]{:S(2)}, u32[]{:S(2)}) collective-permute-start(f32[6,3,4,10,1]{3,2,4,1,0:T(4,128)S(1)} %copy.318), channel_id=1, source_target_pairs={{1,0},{3,2},{5,4},{7,6},{9,8},{11,10},{13,12},{15,14},{17,16},{19,... | collective-permute-start | bytes 8648 | tf_op jit(solution)/shard_map/ppermute | solution.py:24
  255.1 3.1 collective-permute-start.16
  271.5 54.9 %copy-start.1 = (f32[6,16,3]{1,2,0:T(4,128)S(1)}, f32[6,16,3]{1,2,0:T(4,128)}, u32[]{:S(2)}) copy-start(f32[6,16,3]{1,2,0:T(4,128)} %param.17) | copy-start | bytes 3460
where the time goes:
time: 331 us; the launch traced here: 327 us
  blocking collectives  147 us (44%)
  starting transfers between devices  91.8 us (28%)
  other arithmetic  32.8 us (10%)
  matrix products  25.1 us (8%)
  local copies, waits for them, and re-layouts  18.4 us (6%)
  waiting for transfers between devices  8.75 us (3%)
    psum x9, blocking collectives, one_axis_at_a_time(): shard = lax.psum(shard, axis)  147 us
    ppermute x9, starting transfers between devices, padded_2(): lax.ppermute(lax.slice_in_dim(block, 0, width, axis=dim), axis, backward)  58.9 us
    ppermute x9, starting transfers between devices, padded_2(): lax.ppermute(lax.slice_in_dim(block, block.shape[dim] - width, None, axis...  32.9 us
    dot_general x18, matrix products, stiff_apply(): jnp.einsum('ij,jxyz->ixyz', element_stiffness, stacked, precision=highest)  19.1 us
    add x2, other arithmetic, operate(): return inner * forces + (1.0 - inner) * crop(padded, 1)  12.6 us
    ppermute x9, waiting for transfers between devices, padded_2(): lax.ppermute(lax.slice_in_dim(block, block.shape[dim] - width, None, axis...  8.43 us
    unnamed x141, local copies, waits for them, and re-layouts  7.96 us
  transfers between devices with their start and end apart: 18, of which 10 were waited for; matrix products, arithmetic and copies ran while one was open for 2% of the time, Pallas kernels for 0%

commit v1 on v0

v1 whole, which is shorter than its diff:
```python
import functools

import jax
import jax.numpy as jnp
from jax import lax
from jax.experimental import pallas as pl
from jax.experimental.pallas import tpu as pltpu
from jax.sharding import PartitionSpec as P

LEVELS = 16
CASES = 6
LOADS = 16
HALF = 3
soft_modulus = 0.05
poisson_ratio = 0.3
LAM = poisson_ratio / ((1.0 + poisson_ratio) * (1.0 - 2.0 * poisson_ratio))
MU = 1.0 / (2.0 * (1.0 + poisson_ratio))
C11 = LAM + 2.0 * MU
RHO = LAM / MU
KAP = C11 / MU + 1.0
K00 = (C11 + 2.0 * MU) / 9.0
MESH = pl.DeviceIdType.MESH
ANY = pl.ANY
f32 = jnp.float32


def masks():
    lane = lax.broadcasted_iota(jnp.int32, (8, 128), 1)
    sub = lax.broadcasted_iota(jnp.int32, (8, 128), 0)
    return lane, sub


def z_up(v, lane, sub):
    nd = v.ndim
    sh = pltpu.roll(v, 127, axis=nd - 1)
    fx = pltpu.roll(sh, 4, axis=nd - 2)
    return jnp.where(lane == 127, jnp.where(sub < 4, fx, 0.0), sh)


def z_dn(v, lane, sub):
    nd = v.ndim
    sh = pltpu.roll(v, 1, axis=nd - 1)
    fx = pltpu.roll(sh, 4, axis=nd - 2)
    return jnp.where(lane == 0, jnp.where(sub >= 4, fx, 0.0), sh)


def modal(a, em):
    X, Y, Z = 0, 1, 2
    g = {}
    tr = RHO * (a[X, 1, 0, 0] + a[Y, 0, 1, 0] + a[Z, 0, 0, 1])
    for key in ((X, 1, 0, 0), (Y, 0, 1, 0), (Z, 0, 0, 1)):
        g[key] = em * (a[key] + a[key] + tr)
    for p, q in (
        ((X, 0, 1, 0), (Y, 1, 0, 0)),
        ((X, 0, 0, 1), (Z, 1, 0, 0)),
        ((Y, 0, 0, 1), (Z, 0, 1, 0)),
    ):
        g[p] = g[q] = em * (a[p] + a[q])
    e2 = em * (1.0 / 3.0)
    ek = em * (KAP / 3.0)
    er = em * (RHO / 3.0)
    for p, q in (
        ((X, 1, 1, 0), (Z, 0, 1, 1)),
        ((X, 1, 0, 1), (Y, 0, 1, 1)),
        ((Y, 1, 1, 0), (Z, 1, 0, 1)),
    ):
        g[p] = ek * a[p] + er * a[q]
        g[q] = ek * a[q] + er * a[p]
    three = ((X, 0, 1, 1), (Y, 1, 0, 1), (Z, 1, 1, 0))
    total = a[three[0]] + a[three[1]] + a[three[2]]
    for key in three:
        g[key] = e2 * (a[key] + total)
    e3 = em * ((C11 / MU + 2.0) / 9.0)
    for c in range(3):
        g[c, 1, 1, 1] = e3 * a[c, 1, 1, 1]
    return g


def apply_k(node_row, em_row, emit, lane, sub):
    prev_z = None
    prev_hi = None
    for r in range(10):
        zs = []
        for c in range(3):
            v = node_row(c, r)
            w = z_up(v, lane, sub)
            zs.append((v + w, w - v))
        if r > 0:
            a = {}
            for c in range(3):
                for z in (0, 1):
                    lo, hi = prev_z[c][z], zs[c][z]
                    for y, f in ((0, lo + hi), (1, hi - lo)):
                        a[c, 1, y, z] = f[1:4] - f[0:3]
                        if y or z:
                            a[c, 0, y, z] = f[0:3] + f[1:4]
            g = modal(a, em_row(r - 1))
            lows, highs = [], []
            for c in range(3):
                h = {}
                for y in (0, 1):
                    for z in (0, 1):
                        gd = g[c, 1, y, z]
                        t = gd[0:2] - gd[1:3]
                        if y or z:
                            gs = g[c, 0, y, z]
                            t = t + (gs[0:2] + gs[1:3])
                        h[y, z] = t
                lows.append([h[0, z] - h[1, z] for z in (0, 1)])
                highs.append([h[0, z] + h[1, z] for z in (0, 1)])
            if r > 1:
                out = []
                for c in range(3):
                    ks = prev_hi[c][0] + lows[c][0]
                    kd = prev_hi[c][1] + lows[c][1]
                    out.append((ks - kd) + z_dn(ks + kd, lane, sub))
                emit(r - 2, out)
            prev_hi = highs
        prev_z = zs


def cyc1(v, sub):
    return jnp.where(sub % 4 == 2, pltpu.roll(v, 2, axis=v.ndim - 2), pltpu.roll(v, 7, axis=v.ndim - 2))


def cyc2(v, sub):
    return jnp.where(sub % 4 == 0, pltpu.roll(v, 6, axis=v.ndim - 2), pltpu.roll(v, 1, axis=v.ndim - 2))


def pair_products(own_x, other_x, own_y, sub):
    return [
        own_x * own_y,
        cyc1(own_x, sub) * own_y,
        other_x * own_y,
        cyc1(other_x, sub) * own_y,
        cyc2(other_x, sub) * own_y,
    ]


def cholesky(m, n):
    low = {}
    inv = {}
    for j in range(n):
        s = m[j, j]
        for k in range(j):
            s = s - low[j, k] * low[j, k]
        inv[j] = 1.0 / jnp.sqrt(s)
        for i in range(j + 1, n):
            t = m[i, j]
            for k in range(j):
                t = t - low[i, k] * low[j, k]
            low[i, j] = t * inv[j]
    return low, inv


def forward(low, inv, rhs, n):
    out = []
    for i in range(n):
        t = rhs[i]
        for k in range(i):
            t = t - low[i, k] * out[k]
        out.append(t * inv[i])
    return out


def backward(low, inv, rhs, n):
    out = [None] * n
    for i in reversed(range(n)):
        t = rhs[i]
        for k in range(i + 1, n):
            t = t - low[k, i] * out[k]
        out[i] = t * inv[i]
    return out


def kernel(
    nx, ny,
    nodes, vals, x_hbm, b_hbm, d_hbm, s_hbm,
    xo_hbm, ro_hbm,
    xin, bin_, din, sin, xm, ysend, esend, qs,
    nat, yrow, enat, ey, qnat,
    u0, u1, u2, em, mob, scl, rb, ib, yb, ga, ag, bg, xout, rout,
    in_sem, out_sem, ss, rs,
):
    grp, gx, gy, gz = (lax.axis_index(a) for a in ("grp", "gx", "gy", "gz"))
    oz = 1 - gz
    lane, sub = masks()
    valid = sub % 4 < 3
    counter = [0]
    pending = []

    loads = [
        pltpu.make_async_copy(src, dst, in_sem.at[i])
        for i, (src, dst) in enumerate(((d_hbm, din), (s_hbm, sin), (x_hbm, xin), (b_hbm, bin_)))
    ]
    for load in loads:
        load.start()

    barrier = pltpu.get_barrier_semaphore()

    def greet(cx, cy, cz):
        pl.semaphore_signal(barrier, inc=1, device_id=(grp, cx, cy, cz), device_id_type=MESH)

    exists = {}
    for dx in (-1, 0, 1):
        for dy in (-1, 0, 1):
            conds = []
            if dx:
                conds.append(gx > 0 if dx < 0 else gx < nx - 1)
            if dy:
                conds.append(gy > 0 if dy < 0 else gy < ny - 1)
            if conds:
                exists[dx, dy] = functools.reduce(jnp.logical_and, conds)

    greet(gx, gy, oz)
    for d in range(1, ny):
        for core in (0, 1):
            greet(gx, lax.rem(gy + d, ny), core)
    for d in range(1, nx):
        greet(lax.rem(gx + d, nx), gy, gz)
    expected = 1 + 2 * (ny - 1) + (nx - 1)
    extra = 0
    for (dx, dy), here in exists.items():
        cores = ()
        if dx and dy:
            cores = (0, 1)
        elif dx:
            cores = (oz,)
        if cores:

            @pl.when(here)
            def _(dx=dx, dy=dy, cores=cores):
                for core in cores:
                    greet(gx + dx, gy + dy, core)

            extra = extra + len(cores) * here.astype(jnp.int32)

    def clear(ref, *index):
        ref[index] = jnp.zeros(ref[index].shape, f32)

    full = slice(None)

    @pl.when(gx == 0)
    def _():
        clear(nat, pl.ds(0, 3))
        clear(enat, full, 0)
        clear(ey, full, 0)
        for side in (0, 4):
            clear(yrow, side)
        for u in (u1, u2):
            clear(u, full, 0)

    @pl.when(gx == nx - 1)
    def _():
        clear(nat, pl.ds(9, 3))
        for side in (0, 4):
            clear(yrow, side + 3)
        for u in (u1, u2):
            clear(u, full, 3)

    @pl.when(gy == 0)
    def _():
        clear(yrow, pl.ds(0, 4))
        clear(ey)
        for u in (u1, u2):
            clear(u, full, full, 0)

    @pl.when(gy == ny - 1)
    def _():
        clear(yrow, pl.ds(4, 4))
        for u in (u1, u2):
            clear(u, full, full, 9)

    loads[0].wait()
    loads[1].wait()
    mnat = []
    for p in range(2):
        density = (din[p].astype(f32) + 1.0) * (1.0 / LEVELS)
        modulus = soft_modulus + (1.0 - soft_modulus) * density * density * density
        movable = 1.0 - sin[p].astype(f32)
        esend[p] = modulus
        esend[2 + p] = movable
        enat[gz, 1 + p] = modulus
        enat[gz, 3 + p] = movable
        mnat.append(movable)
    loads[2].wait()
    for side in range(2):
        for core in range(2):
            for p in range(2):
                ysend[side, core, p, 8:16] = jnp.zeros((8, 128), f32)
    for case in range(CASES):
        core, k = divmod(case, HALF)
        for comp in range(3):
            for p in range(2):
                t = mnat[p] * xin[case, comp, p]
                xm[core, p * 3 + comp, 8 * k:8 * k + 8] = t
                for side, y in ((0, 0), (1, 7)):
                    ysend[side, core, p, 4 * k + comp:4 * k + comp + 1] = t[y:y + 1]

    pl.semaphore_wait(barrier, expected + extra)

    def view(ref, *index):
        return ref, index

    def descriptor(src, dst, send_index, recv_index, device):
        (a, i), (b, j) = src, dst
        return pltpu.make_async_remote_copy(
            src_ref=a.at[i] if i else a, dst_ref=b.at[j] if j else b,
            send_sem=ss.at[send_index], recv_sem=rs.at[recv_index],
            device_id=device, device_id_type=MESH,
        )

    slots = [0]

    def take(count):
        base = slots[0]
        slots[0] += count
        return base

    def guarded_by(cond, go):
        if cond is None:
            go()
        else:
            pl.when(cond)(go)

    def exchange(cond, items):
        def go():
            for src, dst, index, device in items:
                pending.append((cond, src, dst, counter[0], index, device))
                descriptor(src, dst, counter[0], index, device).start()
                counter[0] += 1

        guarded_by(cond, go)

    def wait_in(cond, ref, index):
        guarded_by(cond, lambda: descriptor(ref, ref, 0, index, partner).wait_recv())

    partner = (grp, gx, gy, oz)

    arrive = []
    half_rows = pl.ds(pl.multiple_of(32 * gz, 8), 24)
    half_16 = pl.ds(pl.multiple_of(16 * gz, 8), 16)
    for dx in (1, -1):
        base = take(2)
        p, slot = (1, 0) if dx > 0 else (0, 3)
        items = [
            (view(xm, core, pl.ds(3 * p, 3)), view(nat, pl.ds(3 * slot, 3), half_rows), base + gz, (grp, gx + dx, gy, core))
            for core in (0, 1)
        ]
        exchange(exists[dx, 0], items)
        for s in (0, 1):
            arrive.append((exists[-dx, 0], view(nat, pl.ds(3 * slot, 3), pl.ds(32 * s, 24)), base + s))
    for dy in (1, -1):
        side, there = (1, 0) if dy > 0 else (0, 1)
        base = take(2)
        items = [
            (view(ysend, side, core), view(yrow, pl.ds(4 * there + 1, 2), half_16), base + gz, (grp, gx, gy + dy, core))
            for core in (0, 1)
        ]
        exchange(exists[0, dy], items)
        for s in (0, 1):
            arrive.append((exists[0, -dy], view(yrow, pl.ds(4 * there + 1, 2), pl.ds(16 * s, 16)), base + s))
        for dx in (1, -1):
            p, slot = (1, 0) if dx > 0 else (0, 3)
            base = take(2)
            items = [
                (view(ysend, side, core, p), view(yrow, 4 * there + slot, half_16), base + gz, (grp, gx + dx, gy + dy, core))
                for core in (0, 1)
            ]
            exchange(exists[dx, dy], items)
            for s in (0, 1):
                arrive.append((exists[-dx, -dy], view(yrow, 4 * there + slot, pl.ds(16 * s, 16)), base + s))
    for (dx, dy), (src, dst) in (
        ((1, 0), ((1, 1), (0, 1))),
        ((0, 1), ((0, 2), (1, 2))),
        ((1, 1), ((1, 1), (0, 1))),
    ):
        base = take(2)
        target = enat if dy == 0 else ey
        items = [
            (view(esend, pl.ds(*src)), view(target, gz, pl.ds(*dst)), base + gz, (grp, gx + dx, gy + dy, core))
            for core in (0, 1)
        ]
        exchange(exists[dx, dy], items)
        for s in (0, 1):
            arrive.append((exists[-dx, -dy], view(target, s, pl.ds(*dst)), base + s))
    other_rows = pl.ds(pl.multiple_of(32 * oz, 8), 24)
    base = take(3)
    exchange(None, [
        (view(xm, oz), view(nat, pl.ds(3, 6), half_rows), base, partner),
        (view(esend), view(enat, gz, pl.ds(1, 4)), base + 1, partner),
    ])
    arrive.append((None, view(nat, pl.ds(3, 6), other_rows), base))
    arrive.append((None, view(enat, oz, pl.ds(1, 4)), base + 1))
    q_slot = base + 2

    loads[3].wait()
    across_z = 128 * 2
    across_y = 8 * ny * across_z
    number = (gy * 8 + sub) * across_z + gz * 128 + lane + (gx * 2) * across_y
    numbers = (number, number + across_y)

    def add_points(l, acc):
        acc = list(acc)
        for case in range(CASES):
            node = nodes[case, l]
            for p in range(2):
                hit = numbers[p] == node
                for comp in range(3):
                    at = (case * 2 + p) * 3 + comp
                    acc[at] = acc[at] + jnp.where(hit, vals[case, 3 * l + comp], 0.0)
        return tuple(acc)

    zero = jnp.zeros((8, 128), f32)
    points = lax.fori_loop(0, LOADS, add_points, (zero,) * (CASES * 6))
    for case in range(CASES):
        core, k = divmod(case, HALF)
        for p in range(2):
            m = mnat[p]
            for comp in range(3):
                total = bin_[case, comp, p] + points[(case * 2 + p) * 3 + comp]
                qs[core, p * 3 + comp, 8 * k:8 * k + 8] = m * total - (1.0 - m) * xin[case, comp, p]
    exchange(None, [(view(qs, oz), view(qnat, full, half_rows), q_slot, partner)])
    for k in range(6):
        nat[3 + k, half_rows] = xm[gz, k]
        qnat[k, half_rows] = qs[gz, k]

    for cond, ref, index in arrive:
        wait_in(cond, ref, index)

    low = sub < 4

    def spread(ref, k, y):
        return jnp.where(low, ref[0, k, y:y + 1], ref[1, k, y:y + 1])

    for j in range(9):
        for e in range(3):
            t = spread(ey, e, 7) if j == 0 else spread(enat, e, j - 1)
            em[j, e] = t * (MU / 16.0)
    for y in range(8):
        rows = em[y] + em[y + 1]
        around = rows[0:2] + rows[1:3]
        esum = (around + z_dn(around, lane, sub)) * (16.0 / MU)
        m = jnp.stack([spread(enat, 3, y), spread(enat, 4, y)])
        guarded = jnp.where(m > 0, esum, 1.0)
        mob[:, 8 * y:8 * y + 8] = m
        scl[:, 8 * y:8 * y + 8] = m / (K00 * guarded) + (1.0 - m)

    for r in range(10):
        for p in range(4):
            for comp in range(3):
                if r == 0:
                    t = yrow[p, pl.ds(comp, 8, stride=4), :]
                elif r == 9:
                    t = yrow[4 + p, pl.ds(comp, 8, stride=4), :]
                else:
                    t = nat[3 * p + comp, pl.ds(r - 1, 8, stride=8), :]
                u0[comp, p, r] = jnp.where(valid, t, 0.0)

    wait_in(None, view(qnat, full, other_rows), q_slot)

    def at(y):
        return pl.ds(8 * y, 8)

    def first(y, force):
        m = mob[:, at(y)]
        s = scl[:, at(y)]
        for comp in range(3):
            q = jnp.stack([qnat[3 * p + comp, pl.ds(y, 8, stride=8), :] for p in range(2)])
            res = jnp.where(valid, q, 0.0) - m * force[comp]
            rb[gz, comp, :, at(y)] = res
            u1[comp, 1:3, 1 + y] = m * (s * res)

    apply_k(lambda c, r: u0[c, :, r], lambda j: em[j], first, lane, sub)

    def swap_halos(u):
        got = []
        for dx in (1, -1):
            src, dst = (2, 0) if dx > 0 else (1, 3)
            base = take(1)
            inner = pl.ds(1, 8)
            exchange(exists[dx, 0], [(view(u, full, src, inner), view(u, full, dst, inner), base, (grp, gx + dx, gy, gz))])
            got.append((exists[-dx, 0], view(u, full, dst, inner), base))
        for dy in (1, -1):
            ysrc, ydst = (8, 0) if dy > 0 else (1, 9)
            base = take(1)
            both = pl.ds(1, 2)
            exchange(exists[0, dy], [(view(u, full, both, ysrc), view(u, full, both, ydst), base, (grp, gx, gy + dy, gz))])
            got.append((exists[0, -dy], view(u, full, both, ydst), base))
            for dx in (1, -1):
                src, dst = (2, 0) if dx > 0 else (1, 3)
                base = take(1)
                exchange(
                    exists[dx, dy],
                    [(view(u, full, src, ysrc), view(u, full, dst, ydst), base, (grp, gx + dx, gy + dy, gz))],
                )
                got.append((exists[-dx, -dy], view(u, full, dst, ydst), base))
        return got

    def share(buf):
        base = take(1)
        exchange(None, [(view(buf, gz), view(buf, gz), base, partner)])
        return (None, view(buf, oz), base)

    got1 = swap_halos(u1)
    got_r = share(rb)
    for item in got1:
        wait_in(*item)

    def second(y, force):
        m = mob[:, at(y)]
        s = scl[:, at(y)]
        for comp in range(3):
            d = s * rb[gz, comp, :, at(y)]
            image = m * force[comp] + (1.0 - m) * d
            ib[gz, comp, :, at(y)] = image
            u2[comp, 1:3, 1 + y] = m * (s * image)

    apply_k(lambda c, r: u1[c, :, r], lambda j: em[j], second, lane, sub)

    got2 = swap_halos(u2)
    got_i = share(ib)
    wait_in(*got_r)
    wait_in(*got_i)

    def grams(make):
        acc = None
        for y in range(8):
            s = scl[:, at(y)]
            for comp in range(3):
                prods = pair_products(*make(comp, y, s), sub)
                acc = prods if acc is None else [a + b for a, b in zip(acc, prods)]
        return [a[0] + a[1] for a in acc]

    def own_other(buf, comp, y):
        return buf[gz, comp, :, at(y)], buf[oz, comp, :, at(y)]

    def make_g(comp, y, s):
        r, ro = own_other(rb, comp, y)
        return s * r, s * ro, ib[gz, comp, :, at(y)]

    def make_h(comp, y, s):
        i, io = own_other(ib, comp, y)
        return i, io, s * i

    def make_p(comp, y, s):
        r, ro = own_other(rb, comp, y)
        return r, ro, s * r

    sums = grams(make_g) + grams(make_h) + grams(make_p)

    for item in got2:
        wait_in(*item)

    jacc = []

    def third(y, force):
        m = mob[:, at(y)]
        s = scl[:, at(y)]
        for comp in range(3):
            i, io = own_other(ib, comp, y)
            w = s * i
            image = m * force[comp] + (1.0 - m) * w
            yb[gz, comp, :, at(y)] = image
            prods = pair_products(w, s * io, image, sub)
            if jacc:
                jacc[0] = [a + b for a, b in zip(jacc[0], prods)]
            else:
                jacc.append(prods)

    apply_k(lambda c, r: u2[c, :, r], lambda j: em[j], third, lane, sub)
    got_y = share(yb)
    sums = sums + [a[0] + a[1] for a in jacc[0]]

    folded = [a + pltpu.roll(a, 4, axis=0) for a in sums]
    ga[pl.ds(80, 48), :] = jnp.zeros((48, 128), f32)
    for t in range(10):
        ga[pl.ds(8 * t, 8), :] = jnp.where(low, folded[2 * t], folded[2 * t + 1])
    row = lax.dot_general(
        jnp.ones((8, 128), f32), ga[...], (((1,), (1,)), ((), ())),
        precision=lax.Precision.HIGHEST, preferred_element_type=f32,
    )
    me = gz * ny + gy
    ag[me] = row[0:1]
    base = take(2 * ny)
    got = []
    for d in range(ny):
        for flip in (0, 1):
            if d == 0 and flip == 0:
                continue
            core = oz if flip else gz
            cy = lax.rem(gy + d, ny)
            index = base + 2 * d + flip
            exchange(None, [(view(ag, me), view(ag, me), index, (grp, gx, cy, core))])
            source = core * ny + lax.rem(gy + ny - d, ny)
            got.append((None, view(ag, source), index))
    for item in got:
        wait_in(*item)
    for s in (0, 1):
        total = ag[s * ny]
        for k in range(1, ny):
            total = total + ag[s * ny + k]
        bg[gx, s:s + 1] = total
    base = take(nx)
    got = []
    for d in range(1, nx):
        exchange(None, [(view(bg, gx), view(bg, gx), base + d, (grp, lax.rem(gx + d, nx), gy, gz))])
        got.append((None, view(bg, lax.rem(gx + nx - d, nx)), base + d))
    for item in got:
        wait_in(*item)
    total = bg[0]
    for k in range(1, nx):
        total = total + bg[k]

    rows = [jnp.broadcast_to(total[s:s + 1], (8, 128)) for s in (0, 1)]

    def entry(matrix, i, j):
        ci, ki = divmod(i, HALF)
        cj, kj = divmod(j, HALF)
        if ci == cj:
            if (ki + 1) % 3 == kj:
                acc, k, s = 1, ki, ci
            elif ki == kj:
                acc, k, s = 0, ki, ci
            else:
                acc, k, s = 1, kj, ci
        else:
            if ci == 1:
                ki, kj = kj, ki
            acc, k, s = 2 + (kj - ki) % 3, ki, 0
        number = matrix * 5 + acc
        where = 8 * (number // 2) + 4 * (number % 2) + k
        return jnp.broadcast_to(rows[s][:, where:where + 1], (8, 128))

    n = CASES
    mats = []
    for matrix in range(4):
        m = {}
        for i in range(n):
            for j in range(i + 1):
                m[i, j] = entry(matrix, i, j)
                m[j, i] = m[i, j]
        mats.append(m)
    mg, mh, mp, mj = mats

    lo1, inv1 = cholesky(mg, n)
    zh = [forward(lo1, inv1, [mh[i, j] for i in range(n)], n) for j in range(n)]
    zp = [forward(lo1, inv1, [mp[i, j] for i in range(n)], n) for j in range(n)]
    th = [backward(lo1, inv1, zh[j], n) for j in range(n)]
    al = [backward(lo1, inv1, zp[j], n) for j in range(n)]
    schur, right = {}, []
    for j in range(n):
        col = []
        for i in range(n):
            t = mg[i, j]
            for k in range(n):
                t = t - zh[i][k] * zp[j][k]
            col.append(t)
            if i >= j:
                t = mj[i, j]
                for k in range(n):
                    t = t - zh[i][k] * zh[j][k]
                schur[i, j] = t
        right.append(col)
    lo2, inv2 = cholesky(schur, n)
    cb = [backward(lo2, inv2, forward(lo2, inv2, right[j], n), n) for j in range(n)]
    ca = []
    for j in range(n):
        col = []
        for i in range(n):
            t = al[j][i]
            for k in range(n):
                t = t - th[k][i] * cb[j][k]
            col.append(t)
        ca.append(col)

    wait_in(*got_y)
    stores = []
    for comp in range(3):
        for p in range(2):
            s = scl[p, pl.ds(4 * gz, 8, stride=8), :]
            fr, fi, fy = [], [], []
            for j in range(n):
                core, k = divmod(j, HALF)
                pick = pl.ds(4 * gz + k, 8, stride=8)
                fr.append(rb[core, comp, p, pick, :])
                fi.append(ib[core, comp, p, pick, :])
                fy.append(yb[core, comp, p, pick, :])
            for i in range(n):
                up = fr[0] * ca[i][0] + fi[0] * cb[i][0]
                dn = fi[0] * ca[i][0] + fy[0] * cb[i][0]
                for j in range(1, n):
                    up = up + fr[j] * ca[i][j] + fi[j] * cb[i][j]
                    dn = dn + fi[j] * ca[i][j] + fy[j] * cb[i][j]
                xout[i, comp, p] = xin[i, comp, p] + s * up
                rout[i, comp, p] = fr[i] - dn
        for k, (src, dst) in enumerate(((xout, xo_hbm), (rout, ro_hbm))):
            c = pltpu.make_async_copy(src.at[:, comp], dst.at[:, comp], out_sem.at[2 * comp + k])
            c.start()
            stores.append(c)
    for cond, *copy in pending:
        guarded_by(cond, lambda: descriptor(*copy).wait_send())
    for c in stores:
        c.wait()


def shards(design, supports, body_load, start, load_nodes, load_values):
    nx, ny = lax.axis_size("gx"), lax.axis_size("gy")
    block = body_load.shape
    vmem = lambda *shape: pltpu.VMEM(shape, f32)
    spec = pl.BlockSpec(memory_space=ANY)
    smem = pl.BlockSpec(memory_space=pltpu.SMEM)
    scratch = [
        vmem(*block), vmem(*block), pltpu.VMEM(design.shape, jnp.int32), pltpu.VMEM(design.shape, jnp.int32),
        vmem(2, 6, 24, 128), vmem(2, 2, 2, 16, 128), vmem(4, 8, 128), vmem(2, 6, 24, 128),
        vmem(12, 64, 128), vmem(8, 32, 128), vmem(2, 5, 8, 128), vmem(2, 3, 8, 128), vmem(6, 64, 128),
        vmem(3, 4, 10, 8, 128), vmem(3, 4, 10, 8, 128), vmem(3, 4, 10, 8, 128),
        vmem(9, 3, 8, 128), vmem(2, 64, 128), vmem(2, 64, 128),
        vmem(2, 3, 2, 64, 128), vmem(2, 3, 2, 64, 128), vmem(2, 3, 2, 64, 128),
        vmem(128, 128), vmem(2 * ny, 1, 128), vmem(nx, 2, 128), vmem(*block), vmem(*block),
        pltpu.SemaphoreType.DMA((4,)), pltpu.SemaphoreType.DMA((6,)),
        pltpu.SemaphoreType.DMA((2 * ny + nx + 64,)), pltpu.SemaphoreType.DMA((2 * ny + nx + 64,)),
    ]
    out = jax.ShapeDtypeStruct(block, f32)
    return pl.pallas_call(
        functools.partial(kernel, nx, ny),
        out_shape=(out, out),
        in_specs=[smem, smem, spec, spec, spec, spec],
        out_specs=(spec, spec),
        scratch_shapes=scratch,
        compiler_params=pltpu.CompilerParams(collective_id=0, has_side_effects=True),
    )(load_nodes, load_values.reshape(CASES, 3 * LOADS), start, body_load, design, supports)


def solution(mesh):
    in_specs = (
        P(("grp", "gx"), "gy", "gz"),
        P(("grp", "gx"), "gy", "gz"),
        P("grp", None, "gx", "gy", "gz"),
        P("grp", None, "gx", "gy", "gz"),
        P("grp", None),
        P("grp", None, None),
    )
    out_specs = (P("grp", None, "gx", "gy", "gz"), P("grp", None, "gx", "gy", "gz"))
    return jax.shard_map(shards, mesh=mesh, in_specs=in_specs, out_specs=out_specs, check_vma=False)
```

time: 331 us -> 89.7 us (0.27); the launches traced: 327 us -> 89.2 us
  blocking collectives: 147 us -> 0 us
  starting transfers between devices: 91.8 us -> 0 us
  Pallas kernels: 0 us -> 84.8 us
  other arithmetic: 32.8 us -> 0 us
  matrix products: 25.1 us -> 0 us
  local copies, waits for them, and re-layouts: 18.4 us -> 3.77 us
  waiting for transfers between devices: 8.75 us -> 0 us
    psum x9 -> x0, blocking collectives: 147 us -> none  [one_axis_at_a_time(): shard = lax.psum(shard, axis)]
    ppermute x18 -> x0, starting transfers between devices: 91.8 us -> none  [the longest x9 58.9 us: padded_2(): lax.ppermute(lax.slice_in_dim(block, 0, width, axis=dim), axis, backward)]
    pallas_call x0 -> x1, Pallas kernels: none -> 84.8 us  [shards(): pl.pallas_call(functools.partial(kernel, nx, ny), out_shape=(out, out), i...]
    dot_general x29 -> x0, matrix products: 24 us -> none  [the longest x18 19.1 us: stiff_apply(): jnp.einsum('ij,jxyz->ixyz', element_stiffness, stacked, precision=highest)]
    add x6 -> x0, other arithmetic: 12.7 us -> none  [the longest x2 12.6 us: operate(): return inner * forces + (1.0 - inner) * crop(padded, 1)]
    ppermute x18 -> x0, waiting for transfers between devices: 8.75 us -> none  [the longest x9 8.43 us: padded_2(): lax.ppermute(lax.slice_in_dim(block, block.shape[dim] - width, None, axis...]
    mul x9 -> x0, other arithmetic: 7.17 us -> none  [the longest x3 4.96 us: stiff_apply(): forces * moduli[None, :span_first - 1, :span_second - 1, :span_third - 1]]
    another operation x14 -> x0, other arithmetic: 5.65 us -> none  [the longest x6 2.42 us: small_solve(): factor = jnp.linalg.cholesky(matrix)]
  transfers between devices with their start and end apart: 18 -> 0, of which waited for: 10 -> 0; matrix products, arithmetic and copies ran while one was open for 2% -> 0% of each run, Pallas kernels for 0% -> 0%
where the time goes in v1:
time: 89.7 us; the launch traced here: 89.2 us
  Pallas kernels  84.8 us (95%)
  local copies, waits for them, and re-layouts  3.77 us (4%)
    pallas_call x1, Pallas kernels, shards(): pl.pallas_call(functools.partial(kernel, nx, ny), out_shape=(out, out), i...  84.8 us
    unnamed x5, local copies, waits for them, and re-layouts  3.1 us

profile of v1, /device:TPU:65, one launch (start us, length us, event | category | flops | bytes accessed | tf_op | source)
XLA Modules:
  0.0 89.2 jit_solution(15080356162500664364)
XLA Ops:
  0.6 0.8 copy.9
  1.4 0.7 reshape.7.vals
  2.1 84.8 %shard_map.77 = (f32[6,3,2,8,128]{4,3,2,1,0:T(8,128)}, f32[6,3,2,8,128]{4,3,2,1,0:T(8,128)}) custom-call(s32[6,16]{1,0:T(8,128)} %nodes.1, f32[6,48]{1,0:T(8,128)} %reshape.7.vals, f32[6,3,2,8,128]{4,3,2,1,0:T(8,128)} %x_hbm.1, f32[6,3,2,8,128]{4,3,2,1,0:T(8,128)} %b_hbm.1, s32[2,8,128]{2,1,0:T(8,128)} %d_hbm.1, s32[2,8,128]{2,1,0:T(8,128)} %s_hbm.1), custom_call_target="tpu_custom_call" | custom-call | tf_op jit(solution)/shard_map/pallas_call | solution.py:725
  86.9 0.0 copy-start
  86.9 1.6 %copy.12 = f32[6,3,2,8,128]{4,3,2,1,0:T(8,128)} copy(f32[6,3,2,8,128]{4,3,2,1,0:T(8,128)} %get-tuple-element.4) | data formatting | bytes 294912
  88.5 0.0 copy-done
  88.5 0.7 copy.13
Async XLA Ops:
  86.9 1.6 %copy-start = (f32[6,3,2,8,128]{4,3,2,1,0:T(8,128)S(1)}, f32[6,3,2,8,128]{4,3,2,1,0:T(8,128)}, u32[]{:S(2)}) copy-start(f32[6,3,2,8,128]{4,3,2,1,0:T(8,128)} %get-tuple-element.5) | copy-start | bytes 442372

commit v2 on v1

--- a/solution.py
+++ b/solution.py
@@ -20,7 +20,6 @@
 KAP = C11 / MU + 1.0
 K00 = (C11 + 2.0 * MU) / 9.0
 MESH = pl.DeviceIdType.MESH
-ANY = pl.ANY
 f32 = jnp.float32
 
 
@@ -175,23 +174,32 @@
 
 def kernel(
     nx, ny,
-    nodes, vals, x_hbm, b_hbm, d_hbm, s_hbm,
+    n_hbm, v_hbm, x_hbm, b_hbm, d_hbm, s_hbm,
     xo_hbm, ro_hbm,
     xin, bin_, din, sin, xm, ysend, esend, qs,
     nat, yrow, enat, ey, qnat,
-    u0, u1, u2, em, mob, scl, rb, ib, yb, ga, ag, bg, xout, rout,
-    in_sem, out_sem, ss, rs,
+    u0, u1, u2, em, mob, scl, rb, ib, yb, ga, ag, bg, dummy, xout, rout, nodes, vals,
+    in_sem, out_sem, ss, rs, heard,
 ):
     grp, gx, gy, gz = (lax.axis_index(a) for a in ("grp", "gx", "gy", "gz"))
     oz = 1 - gz
     lane, sub = masks()
     valid = sub % 4 < 3
-    counter = [0]
-    pending = []
+    scope = [None]
+
+    def mark(name):
+        if scope[0] is not None:
+            scope[0].__exit__(None, None, None)
+        scope[0] = None
+        if name is not None:
+            scope[0] = jax.named_scope(name)
+            scope[0].__enter__()
+
+    mark('entry')
 
     loads = [
         pltpu.make_async_copy(src, dst, in_sem.at[i])
-        for i, (src, dst) in enumerate(((d_hbm, din), (s_hbm, sin), (x_hbm, xin), (b_hbm, bin_)))
+        for i, (src, dst) in enumerate(((d_hbm, din), (s_hbm, sin), (x_hbm, xin), (b_hbm, bin_), (n_hbm, nodes), (v_hbm, vals)))
     ]
     for load in loads:
         load.start()
@@ -213,27 +221,33 @@
                 exists[dx, dy] = functools.reduce(jnp.logical_and, conds)
 
     greet(gx, gy, oz)
-    for d in range(1, ny):
-        for core in (0, 1):
-            greet(gx, lax.rem(gy + d, ny), core)
-    for d in range(1, nx):
-        greet(lax.rem(gx + d, nx), gy, gz)
-    expected = 1 + 2 * (ny - 1) + (nx - 1)
-    extra = 0
+    expected = 1
     for (dx, dy), here in exists.items():
-        cores = ()
-        if dx and dy:
-            cores = (0, 1)
-        elif dx:
-            cores = (oz,)
-        if cores:
+
+        @pl.when(here)
+        def _(dx=dx, dy=dy):
+            for core in (0, 1):
+                greet(gx + dx, gy + dy, core)
+
+        expected = expected + 2 * here.astype(jnp.int32)
+
+    def round_of(number):
+        step = 2**number
+        for size, mine, place in ((nx, gx, lambda c: (c, gy)), (ny, gy, lambda c: (gx, c))):
+            if step < size:
+                for d in (step, -step):
+                    yield (mine + d < size if d > 0 else mine + d >= 0), place(mine + d)
+
+    def tell(number):
+        for here, (cx, cy) in round_of(number):
 
             @pl.when(here)
-            def _(dx=dx, dy=dy, cores=cores):
-                for core in cores:
-                    greet(gx + dx, gy + dy, core)
-
-            extra = extra + len(cores) * here.astype(jnp.int32)
+            def _(cx=cx, cy=cy):
+                pl.semaphore_signal(heard.at[number], inc=1, device_id=(grp, cx, cy, gz), device_id_type=MESH)
+
+    def hear(number):
+        count = sum(here.astype(jnp.int32) for here, _ in round_of(number))
+        pl.semaphore_wait(heard.at[number], count)
 
     def clear(ref, *index):
         ref[index] = jnp.zeros(ref[index].shape, f32)
@@ -271,6 +285,7 @@
         for u in (u1, u2):
             clear(u, full, full, 9)
 
+    mark('prep')
     loads[0].wait()
     loads[1].wait()
     mnat = []
@@ -297,7 +312,10 @@
                 for side, y in ((0, 0), (1, 7)):
                     ysend[side, core, p, 4 * k + comp:4 * k + comp + 1] = t[y:y + 1]
 
-    pl.semaphore_wait(barrier, expected + extra)
+    mark('barrier')
+    pl.semaphore_wait(barrier, expected)
+    tell(0)
+    mark('send1')
 
     def view(ref, *index):
         return ref, index
@@ -310,91 +328,70 @@
             device_id=device, device_id_type=MESH,
         )
 
-    slots = [0]
-
-    def take(count):
-        base = slots[0]
-        slots[0] += count
-        return base
-
     def guarded_by(cond, go):
         if cond is None:
             go()
         else:
             pl.when(cond)(go)
 
-    def exchange(cond, items):
+    def exchange(cond, send_index, recv_index, items):
         def go():
-            for src, dst, index, device in items:
-                pending.append((cond, src, dst, counter[0], index, device))
-                descriptor(src, dst, counter[0], index, device).start()
-                counter[0] += 1
+            for src, dst, device in items:
+                descriptor(src, dst, send_index, recv_index, device).start()
 
         guarded_by(cond, go)
 
-    def wait_in(cond, ref, index):
+    def wait_in(cond, index, ref):
         guarded_by(cond, lambda: descriptor(ref, ref, 0, index, partner).wait_recv())
 
+    def wait_out(cond, index, ref):
+        guarded_by(cond, lambda: descriptor(ref, ref, index, 0, partner).wait_send())
+
+    def rows_of(count):
+        return view(dummy, pl.ds(0, count))
+
+    slot = {key: i for i, key in enumerate(exists)}
     partner = (grp, gx, gy, oz)
 
-    arrive = []
     half_rows = pl.ds(pl.multiple_of(32 * gz, 8), 24)
     half_16 = pl.ds(pl.multiple_of(16 * gz, 8), 16)
-    for dx in (1, -1):
-        base = take(2)
-        p, slot = (1, 0) if dx > 0 else (0, 3)
-        items = [
-            (view(xm, core, pl.ds(3 * p, 3)), view(nat, pl.ds(3 * slot, 3), half_rows), base + gz, (grp, gx + dx, gy, core))
-            for core in (0, 1)
-        ]
-        exchange(exists[dx, 0], items)
-        for s in (0, 1):
-            arrive.append((exists[-dx, 0], view(nat, pl.ds(3 * slot, 3), pl.ds(32 * s, 24)), base + s))
-    for dy in (1, -1):
+    other_rows = pl.ds(pl.multiple_of(32 * oz, 8), 24)
+    bytes1 = {}
+    for key in sorted(exists, key=lambda k: abs(k[1])):
+        dx, dy = key
+        items, count = [], 0
+        p, there_p = (1, 0) if dx > 0 else (0, 3)
         side, there = (1, 0) if dy > 0 else (0, 1)
-        base = take(2)
-        items = [
-            (view(ysend, side, core), view(yrow, pl.ds(4 * there + 1, 2), half_16), base + gz, (grp, gx, gy + dy, core))
-            for core in (0, 1)
-        ]
-        exchange(exists[0, dy], items)
-        for s in (0, 1):
-            arrive.append((exists[0, -dy], view(yrow, pl.ds(4 * there + 1, 2), pl.ds(16 * s, 16)), base + s))
-        for dx in (1, -1):
-            p, slot = (1, 0) if dx > 0 else (0, 3)
-            base = take(2)
-            items = [
-                (view(ysend, side, core, p), view(yrow, 4 * there + slot, half_16), base + gz, (grp, gx + dx, gy + dy, core))
-                for core in (0, 1)
-            ]
-            exchange(exists[dx, dy], items)
-            for s in (0, 1):
-                arrive.append((exists[-dx, -dy], view(yrow, 4 * there + slot, pl.ds(16 * s, 16)), base + s))
-    for (dx, dy), (src, dst) in (
-        ((1, 0), ((1, 1), (0, 1))),
-        ((0, 1), ((0, 2), (1, 2))),
-        ((1, 1), ((1, 1), (0, 1))),
-    ):
-        base = take(2)
-        target = enat if dy == 0 else ey
-        items = [
-            (view(esend, pl.ds(*src)), view(target, gz, pl.ds(*dst)), base + gz, (grp, gx + dx, gy + dy, core))
-            for core in (0, 1)
-        ]
-        exchange(exists[dx, dy], items)
-        for s in (0, 1):
-            arrive.append((exists[-dx, -dy], view(target, s, pl.ds(*dst)), base + s))
-    other_rows = pl.ds(pl.multiple_of(32 * oz, 8), 24)
-    base = take(3)
-    exchange(None, [
-        (view(xm, oz), view(nat, pl.ds(3, 6), half_rows), base, partner),
-        (view(esend), view(enat, gz, pl.ds(1, 4)), base + 1, partner),
+        for core in (0, 1):
+            device = (grp, gx + dx, gy + dy, core)
+            if dy == 0:
+                items.append((view(xm, core, pl.ds(3 * p, 3)), view(nat, pl.ds(3 * there_p, 3), half_rows), device))
+                count += 72
+                if dx > 0:
+                    items.append((view(esend, pl.ds(1, 1)), view(enat, gz, pl.ds(0, 1)), device))
+                    count += 8
+            elif dx == 0:
+                items.append((view(ysend, side, core), view(yrow, pl.ds(4 * there + 1, 2), half_16), device))
+                count += 32
+                if dy > 0:
+                    items.append((view(esend, pl.ds(0, 2)), view(ey, gz, pl.ds(1, 2)), device))
+                    count += 16
+            else:
+                items.append((view(ysend, side, core, p), view(yrow, 4 * there + there_p, half_16), device))
+                count += 16
+                if dx > 0 and dy > 0:
+                    items.append((view(esend, pl.ds(1, 1)), view(ey, gz, pl.ds(0, 1)), device))
+                    count += 8
+        exchange(exists[key], slot[key], slot[key], items)
+        bytes1[key] = count
+    exchange(None, 8, 16, [
+        (view(xm, oz), view(nat, pl.ds(3, 6), half_rows), partner),
+        (view(esend), view(enat, gz, pl.ds(1, 4)), partner),
     ])
-    arrive.append((None, view(nat, pl.ds(3, 6), other_rows), base))
-    arrive.append((None, view(enat, oz, pl.ds(1, 4)), base + 1))
-    q_slot = base + 2
-
-    loads[3].wait()
+
+    mark('points')
+    for load in loads[3:]:
+        load.wait()
     across_z = 128 * 2
     across_y = 8 * ny * across_z
     number = (gy * 8 + sub) * across_z + gz * 128 + lane + (gx * 2) * across_y
@@ -408,7 +405,7 @@
                 hit = numbers[p] == node
                 for comp in range(3):
                     at = (case * 2 + p) * 3 + comp
-                    acc[at] = acc[at] + jnp.where(hit, vals[case, 3 * l + comp], 0.0)
+                    acc[at] = acc[at] + jnp.where(hit, vals[case, comp, l], 0.0)
         return tuple(acc)
 
     zero = jnp.zeros((8, 128), f32)
@@ -420,13 +417,20 @@
             for comp in range(3):
                 total = bin_[case, comp, p] + points[(case * 2 + p) * 3 + comp]
                 qs[core, p * 3 + comp, 8 * k:8 * k + 8] = m * total - (1.0 - m) * xin[case, comp, p]
-    exchange(None, [(view(qs, oz), view(qnat, full, half_rows), q_slot, partner)])
+    exchange(None, 9, 17, [(view(qs, oz), view(qnat, full, half_rows), partner)])
     for k in range(6):
         nat[3 + k, half_rows] = xm[gz, k]
         qnat[k, half_rows] = qs[gz, k]
 
-    for cond, ref, index in arrive:
-        wait_in(cond, ref, index)
+    hear(0)
+    tell(1)
+    mark('wait1')
+    for (dx, dy), index in slot.items():
+        wait_in(exists[-dx, -dy], index, rows_of(bytes1[dx, dy]))
+    wait_in(None, 16, rows_of(176))
+    hear(1)
+    tell(2)
+    mark('build')
 
     low = sub < 4
 
@@ -457,7 +461,9 @@
                     t = nat[3 * p + comp, pl.ds(r - 1, 8, stride=8), :]
                 u0[comp, p, r] = jnp.where(valid, t, 0.0)
 
-    wait_in(None, view(qnat, full, other_rows), q_slot)
+    mark('waitq')
+    wait_in(None, 17, view(qnat, full, other_rows))
+    mark('k1')
 
     def at(y):
         return pl.ds(8 * y, 8)
@@ -473,39 +479,45 @@
 
     apply_k(lambda c, r: u0[c, :, r], lambda j: em[j], first, lane, sub)
 
-    def swap_halos(u):
-        got = []
-        for dx in (1, -1):
-            src, dst = (2, 0) if dx > 0 else (1, 3)
-            base = take(1)
-            inner = pl.ds(1, 8)
-            exchange(exists[dx, 0], [(view(u, full, src, inner), view(u, full, dst, inner), base, (grp, gx + dx, gy, gz))])
-            got.append((exists[-dx, 0], view(u, full, dst, inner), base))
-        for dy in (1, -1):
-            ysrc, ydst = (8, 0) if dy > 0 else (1, 9)
-            base = take(1)
-            both = pl.ds(1, 2)
-            exchange(exists[0, dy], [(view(u, full, both, ysrc), view(u, full, both, ydst), base, (grp, gx, gy + dy, gz))])
-            got.append((exists[0, -dy], view(u, full, both, ydst), base))
-            for dx in (1, -1):
-                src, dst = (2, 0) if dx > 0 else (1, 3)
-                base = take(1)
-                exchange(
-                    exists[dx, dy],
-                    [(view(u, full, src, ysrc), view(u, full, dst, ydst), base, (grp, gx + dx, gy + dy, gz))],
-                )
-                got.append((exists[-dx, -dy], view(u, full, dst, ydst), base))
-        return got
-
-    def share(buf):
-        base = take(1)
-        exchange(None, [(view(buf, gz), view(buf, gz), base, partner)])
-        return (None, view(buf, oz), base)
-
-    got1 = swap_halos(u1)
-    got_r = share(rb)
-    for item in got1:
-        wait_in(*item)
+    def halo_views(u, key):
+        dx, dy = key
+        src, dst = (2, 0) if dx > 0 else (1, 3)
+        ysrc, ydst = (8, 0) if dy > 0 else (1, 9)
+        if dy == 0:
+            return view(u, full, src, pl.ds(1, 8)), view(u, full, dst, pl.ds(1, 8))
+        if dx == 0:
+            return view(u, full, pl.ds(1, 2), ysrc), view(u, full, pl.ds(1, 2), ydst)
+        return view(u, full, src, ysrc), view(u, full, dst, ydst)
+
+    def swap_halos(u, first_slot):
+        for key in sorted(exists, key=lambda k: abs(k[1])):
+            dx, dy = key
+            exchange(
+                exists[key], slot[key], first_slot + slot[key],
+                [(*halo_views(u, key), (grp, gx + dx, gy + dy, gz))],
+            )
+
+    def take_halos(u, first_slot):
+        for dx, dy in exists:
+            wait_in(exists[-dx, -dy], first_slot + slot[dx, dy], halo_views(u, (dx, dy))[1])
+
+    def sent_halos(u):
+        for key in exists:
+            wait_out(exists[key], slot[key], halo_views(u, key)[0])
+
+    def share(buf, send_index, recv_index):
+        exchange(None, send_index, recv_index, [(view(buf, gz), view(buf, gz), partner)])
+
+    for key in exists:
+        wait_out(exists[key], slot[key], rows_of(bytes1[key]))
+    wait_out(None, 8, rows_of(176))
+    swap_halos(u1, 8)
+    share(rb, 8, 18)
+    mark('wait2')
+    take_halos(u1, 8)
+    hear(2)
+    tell(3)
+    mark('k2')
 
     def second(y, force):
         m = mob[:, at(y)]
@@ -518,11 +530,15 @@
 
     apply_k(lambda c, r: u1[c, :, r], lambda j: em[j], second, lane, sub)
 
-    got2 = swap_halos(u2)
-    got_i = share(ib)
-    wait_in(*got_r)
-    wait_in(*got_i)
-
+    mark('send3')
+    sent_halos(u1)
+    wait_out(None, 9, view(qs, oz))
+    swap_halos(u2, 0)
+    share(ib, 9, 19)
+    wait_in(None, 18, view(rb, oz))
+    wait_in(None, 19, view(ib, oz))
+
+    mark('grams')
     def grams(make):
         acc = None
         for y in range(8):
@@ -549,8 +565,9 @@
 
     sums = grams(make_g) + grams(make_h) + grams(make_p)
 
-    for item in got2:
-        wait_in(*item)
+    mark('wait3')
+    take_halos(u2, 0)
+    mark('k3')
 
     jacc = []
 
@@ -569,9 +586,11 @@
                 jacc.append(prods)
 
     apply_k(lambda c, r: u2[c, :, r], lambda j: em[j], third, lane, sub)
-    got_y = share(yb)
+    wait_out(None, 8, view(rb, gz))
+    share(yb, 8, 20)
     sums = sums + [a[0] + a[1] for a in jacc[0]]
 
+    mark('rowsum')
     folded = [a + pltpu.roll(a, 4, axis=0) for a in sums]
     ga[pl.ds(80, 48), :] = jnp.zeros((48, 128), f32)
     for t in range(10):
@@ -580,34 +599,26 @@
         jnp.ones((8, 128), f32), ga[...], (((1,), (1,)), ((), ())),
         precision=lax.Precision.HIGHEST, preferred_element_type=f32,
     )
+    mark('reduce_a')
     me = gz * ny + gy
     ag[me] = row[0:1]
-    base = take(2 * ny)
-    got = []
-    for d in range(ny):
-        for flip in (0, 1):
-            if d == 0 and flip == 0:
-                continue
-            core = oz if flip else gz
-            cy = lax.rem(gy + d, ny)
-            index = base + 2 * d + flip
-            exchange(None, [(view(ag, me), view(ag, me), index, (grp, gx, cy, core))])
-            source = core * ny + lax.rem(gy + ny - d, ny)
-            got.append((None, view(ag, source), index))
-    for item in got:
-        wait_in(*item)
+    exchange(None, 10, 21, [
+        (view(ag, me), view(ag, me), (grp, gx, lax.rem(gy + d, ny), oz if flip else gz))
+        for d in range(ny) for flip in (0, 1) if d or flip
+    ])
+    wait_in(None, 21, view(ag, pl.ds(0, 2 * ny - 1)))
     for s in (0, 1):
         total = ag[s * ny]
         for k in range(1, ny):
             total = total + ag[s * ny + k]
         bg[gx, s:s + 1] = total
-    base = take(nx)
-    got = []
-    for d in range(1, nx):
-        exchange(None, [(view(bg, gx), view(bg, gx), base + d, (grp, lax.rem(gx + d, nx), gy, gz))])
-        got.append((None, view(bg, lax.rem(gx + nx - d, nx)), base + d))
-    for item in got:
-        wait_in(*item)
+    hear(3)
+    mark('reduce_b')
+    exchange(None, 11, 22, [
+        (view(bg, gx), view(bg, gx), (grp, lax.rem(gx + d, nx), gy, gz)) for d in range(1, nx)
+    ])
+    wait_in(None, 22, view(bg, pl.ds(0, nx - 1)))
+    mark('solve')
     total = bg[0]
     for k in range(1, nx):
         total = total + bg[k]
@@ -674,8 +685,8 @@
             col.append(t)
         ca.append(col)
 
-    wait_in(*got_y)
-    stores = []
+    mark('combine')
+    wait_in(None, 20, view(yb, oz))
     for comp in range(3):
         for p in range(2):
             s = scl[p, pl.ds(4 * gz, 8, stride=8), :]
@@ -694,22 +705,24 @@
                     dn = dn + fi[j] * ca[i][j] + fy[j] * cb[i][j]
                 xout[i, comp, p] = xin[i, comp, p] + s * up
                 rout[i, comp, p] = fr[i] - dn
-        for k, (src, dst) in enumerate(((xout, xo_hbm), (rout, ro_hbm))):
-            c = pltpu.make_async_copy(src.at[:, comp], dst.at[:, comp], out_sem.at[2 * comp + k])
-            c.start()
-            stores.append(c)
-    for cond, *copy in pending:
-        guarded_by(cond, lambda: descriptor(*copy).wait_send())
-    for c in stores:
-        c.wait()
+        for i, (src, dst) in enumerate(((xout, xo_hbm), (rout, ro_hbm))):
+            pltpu.make_async_copy(src.at[:, comp], dst.at[:, comp], out_sem.at[i]).start()
+    mark('drain')
+    sent_halos(u2)
+    wait_out(None, 8, view(yb, gz))
+    wait_out(None, 9, view(ib, gz))
+    wait_out(None, 10, view(ag, pl.ds(0, 2 * ny - 1)))
+    wait_out(None, 11, view(bg, pl.ds(0, nx - 1)))
+    for i, (src, dst) in enumerate(((xout, xo_hbm), (rout, ro_hbm))):
+        pltpu.make_async_copy(src, dst, out_sem.at[i]).wait()
+    mark(None)
 
 
 def shards(design, supports, body_load, start, load_nodes, load_values):
     nx, ny = lax.axis_size("gx"), lax.axis_size("gy")
     block = body_load.shape
     vmem = lambda *shape: pltpu.VMEM(shape, f32)
-    spec = pl.BlockSpec(memory_space=ANY)
-    smem = pl.BlockSpec(memory_space=pltpu.SMEM)
+    spec = pl.BlockSpec(memory_space=pl.ANY)
     scratch = [
         vmem(*block), vmem(*block), pltpu.VMEM(design.shape, jnp.int32), pltpu.VMEM(design.shape, jnp.int32),
         vmem(2, 6, 24, 128), vmem(2, 2, 2, 16, 128), vmem(4, 8, 128), vmem(2, 6, 24, 128),
@@ -717,19 +730,20 @@
         vmem(3, 4, 10, 8, 128), vmem(3, 4, 10, 8, 128), vmem(3, 4, 10, 8, 128),
         vmem(9, 3, 8, 128), vmem(2, 64, 128), vmem(2, 64, 128),
         vmem(2, 3, 2, 64, 128), vmem(2, 3, 2, 64, 128), vmem(2, 3, 2, 64, 128),
-        vmem(128, 128), vmem(2 * ny, 1, 128), vmem(nx, 2, 128), vmem(*block), vmem(*block),
-        pltpu.SemaphoreType.DMA((4,)), pltpu.SemaphoreType.DMA((6,)),
-        pltpu.SemaphoreType.DMA((2 * ny + nx + 64,)), pltpu.SemaphoreType.DMA((2 * ny + nx + 64,)),
+        vmem(128, 128), vmem(2 * ny, 1, 128), vmem(nx, 2, 128), vmem(176, 128), vmem(*block), vmem(*block),
+        pltpu.SMEM(load_nodes.shape, jnp.int32), pltpu.SMEM((CASES, 3, LOADS), f32),
+        pltpu.SemaphoreType.DMA((6,)), pltpu.SemaphoreType.DMA((2,)), pltpu.SemaphoreType.DMA((12,)), pltpu.SemaphoreType.DMA((23,)),
+        pltpu.SemaphoreType.REGULAR((4,)),
     ]
     out = jax.ShapeDtypeStruct(block, f32)
     return pl.pallas_call(
         functools.partial(kernel, nx, ny),
         out_shape=(out, out),
-        in_specs=[smem, smem, spec, spec, spec, spec],
+        in_specs=[spec] * 6,
         out_specs=(spec, spec),
         scratch_shapes=scratch,
         compiler_params=pltpu.CompilerParams(collective_id=0, has_side_effects=True),
-    )(load_nodes, load_values.reshape(CASES, 3 * LOADS), start, body_load, design, supports)
+    )(load_nodes, jnp.transpose(load_values, (0, 2, 1)), start, body_load, design, supports)
 
 
 def solution(mesh):

time: 89.7 us -> 80.6 us (0.90)
  Pallas kernels: 84.8 us -> 77.4 us
  local copies, waits for them, and re-layouts: 3.77 us -> 2.28 us
    pallas_call x1, Pallas kernels: 84.8 us -> 77.4 us  [shards(): pl.pallas_call(functools.partial(kernel, nx, ny), out_shape=(out, out), i...]
    unnamed x5 -> x4, local copies, waits for them, and re-layouts: 3.1 us -> 2.28 us
where the time goes in v2:
time: 80.6 us; the launch traced here: 80.3 us
  Pallas kernels  77.4 us (96%)
  local copies, waits for them, and re-layouts  2.28 us (3%)
    pallas_call x1, Pallas kernels, shards(): pl.pallas_call(functools.partial(kernel, nx, ny), out_shape=(out, out), i...  77.4 us
    unnamed x4, local copies, waits for them, and re-layouts  2.28 us

profile of v2, /device:TPU:65, one launch (start us, length us, event | category | flops | bytes accessed | tf_op | source)
XLA Modules:
  0.0 80.3 jit_solution(16256969524012559085)
XLA Ops:
  0.6 77.4 %shard_map.77 = (f32[6,3,2,8,128]{4,3,2,1,0:T(8,128)}, f32[6,3,2,8,128]{4,3,2,1,0:T(8,128)}) custom-call(s32[6,16]{1,0:T(8,128)} %n_hbm.1, f32[6,3,16]{2,1,0:T(4,128)} %bitcast.1, f32[6,3,2,8,128]{4,3,2,1,0:T(8,128)} %x_hbm.1, f32[6,3,2,8,128]{4,3,2,1,0:T(8,128)} %b_hbm.1, s32[2,8,128]{2,1,0:T(8,128)} %d_hbm.1, s32[2,8,128]{2,1,0:T(8,128)} %s_hbm.1), custom_call_target="tpu_custom_call" | custom-call | tf_op jit(solution)/shard_map/pallas_call | solution.py:739
  78.0 0.0 copy-start
  78.0 1.6 %copy.10 = f32[6,3,2,8,128]{4,3,2,1,0:T(8,128)} copy(f32[6,3,2,8,128]{4,3,2,1,0:T(8,128)} %get-tuple-element.4) | data formatting | bytes 294912
  79.7 0.0 copy-done
  79.7 0.7 copy.11
Async XLA Ops:
  78.0 1.6 %copy-start = (f32[6,3,2,8,128]{4,3,2,1,0:T(8,128)S(1)}, f32[6,3,2,8,128]{4,3,2,1,0:T(8,128)}, u32[]{:S(2)}) copy-start(f32[6,3,2,8,128]{4,3,2,1,0:T(8,128)} %get-tuple-element.5) | copy-start | bytes 442372

commit v3 on v2

--- a/solution.py
+++ b/solution.py
@@ -357,7 +357,7 @@
     half_16 = pl.ds(pl.multiple_of(16 * gz, 8), 16)
     other_rows = pl.ds(pl.multiple_of(32 * oz, 8), 24)
     bytes1 = {}
-    for key in sorted(exists, key=lambda k: abs(k[1])):
+    for key in sorted(exists, key=lambda k: (k[1] == 0, -abs(k[0]))):
         dx, dy = key
         items, count = [], 0
         p, there_p = (1, 0) if dx > 0 else (0, 3)
@@ -484,26 +484,44 @@
         src, dst = (2, 0) if dx > 0 else (1, 3)
         ysrc, ydst = (8, 0) if dy > 0 else (1, 9)
         if dy == 0:
-            return view(u, full, src, pl.ds(1, 8)), view(u, full, dst, pl.ds(1, 8))
+            return [(view(u, full, src, pl.ds(k, 3)), view(u, full, dst, pl.ds(k, 3))) for k in (1, 5)]
         if dx == 0:
-            return view(u, full, pl.ds(1, 2), ysrc), view(u, full, pl.ds(1, 2), ydst)
-        return view(u, full, src, ysrc), view(u, full, dst, ydst)
+            return [(view(u, full, pl.ds(1, 2), ysrc), view(u, full, pl.ds(1, 2), ydst))]
+        return [(view(u, full, src, ysrc), view(u, full, dst, ydst))]
+
+    halo_rows = {(dx, dy): 8 * 3 * (6 if dy == 0 else 2 if dx == 0 else 1) for dx, dy in exists}
+
+    free = sub % 4 == 3
+
+    def pack(u):
+        for k in (0, 4):
+            t = u[:, 1:3, k + 4]
+            for i in (1, 2, 3):
+                u[:, 1:3, k + i] = jnp.where(free, pltpu.roll(t, 4 - i, axis=2), u[:, 1:3, k + i])
+
+    def unpack(u):
+        for p in (0, 3):
+            for k in (0, 4):
+                a, b, c = (pltpu.roll(u[:, p, k + i], 4 + i, axis=1) for i in (1, 2, 3))
+                u[:, p, k + 4] = jnp.where(sub % 4 == 0, a, jnp.where(sub % 4 == 1, b, c))
 
     def swap_halos(u, first_slot):
-        for key in sorted(exists, key=lambda k: abs(k[1])):
+        pack(u)
+        for key in sorted(exists, key=lambda k: (k[1] == 0, -abs(k[0]))):
             dx, dy = key
             exchange(
                 exists[key], slot[key], first_slot + slot[key],
-                [(*halo_views(u, key), (grp, gx + dx, gy + dy, gz))],
+                [(a, b, (grp, gx + dx, gy + dy, gz)) for a, b in halo_views(u, key)],
             )
 
     def take_halos(u, first_slot):
         for dx, dy in exists:
-            wait_in(exists[-dx, -dy], first_slot + slot[dx, dy], halo_views(u, (dx, dy))[1])
+            wait_in(exists[-dx, -dy], first_slot + slot[dx, dy], rows_of(halo_rows[dx, dy]))
+        unpack(u)
 
     def sent_halos(u):
         for key in exists:
-            wait_out(exists[key], slot[key], halo_views(u, key)[0])
+            wait_out(exists[key], slot[key], rows_of(halo_rows[key]))
 
     def share(buf, send_index, recv_index):
         exchange(None, send_index, recv_index, [(view(buf, gz), view(buf, gz), partner)])
@@ -703,8 +721,8 @@
                 for j in range(1, n):
                     up = up + fr[j] * ca[i][j] + fi[j] * cb[i][j]
                     dn = dn + fi[j] * ca[i][j] + fy[j] * cb[i][j]
-                xout[i, comp, p] = xin[i, comp, p] + s * up
-                rout[i, comp, p] = fr[i] - dn
+                xout[i, comp, p] = s * up
+                rout[i, comp, p] = (fr[i] - dn) + xin[i, comp, p]
         for i, (src, dst) in enumerate(((xout, xo_hbm), (rout, ro_hbm))):
             pltpu.make_async_copy(src.at[:, comp], dst.at[:, comp], out_sem.at[i]).start()
     mark('drain')
@@ -736,7 +754,7 @@
         pltpu.SemaphoreType.REGULAR((4,)),
     ]
     out = jax.ShapeDtypeStruct(block, f32)
-    return pl.pallas_call(
+    change, shifted = pl.pallas_call(
         functools.partial(kernel, nx, ny),
         out_shape=(out, out),
         in_specs=[spec] * 6,
@@ -744,6 +762,8 @@
         scratch_shapes=scratch,
         compiler_params=pltpu.CompilerParams(collective_id=0, has_side_effects=True),
     )(load_nodes, jnp.transpose(load_values, (0, 2, 1)), start, body_load, design, supports)
+
+    return start + change, shifted - start
 
 
 def solution(mesh):

time: 80.6 us -> 76.7 us (0.952)
  Pallas kernels: 77.4 us -> 74.2 us
  local copies, waits for them, and re-layouts: 2.28 us -> 0.01 us
  other arithmetic: 0 us -> 1.72 us
    pallas_call x1, Pallas kernels: 77.4 us -> 74.2 us  [shards(): pl.pallas_call(functools.partial(kernel, nx, ny), out_shape=(out, out), i...]
    unnamed x4 -> x2, local copies, waits for them, and re-layouts: 2.28 us -> 0.01 us
    sub x0 -> x1, other arithmetic: none -> 1.72 us  [shards(): return (start + change, shifted - start)]
where the time goes in v3:
time: 76.7 us; the launch traced here: 76.5 us
  Pallas kernels  74.2 us (97%)
  other arithmetic  1.72 us (2%)
    pallas_call x1, Pallas kernels, shards(): pl.pallas_call(functools.partial(kernel, nx, ny), out_shape=(out, out), i...  74.2 us
    sub x1, other arithmetic, shards(): return (start + change, shifted - start)  1.72 us

profile of v3, /device:TPU:65, one launch (start us, length us, event | category | flops | bytes accessed | tf_op | source)
XLA Modules:
  0.0 76.5 jit_solution(16237851618917990288)
XLA Ops:
  0.6 0.0 copy-start
  0.6 74.2 %shard_map.77 = (f32[6,3,2,8,128]{4,3,2,1,0:T(8,128)}, f32[6,3,2,8,128]{4,3,2,1,0:T(8,128)}) custom-call(s32[6,16]{1,0:T(8,128)} %n_hbm.1, f32[6,3,16]{2,1,0:T(4,128)} %bitcast.1, f32[6,3,2,8,128]{4,3,2,1,0:T(8,128)} %x_hbm.1, f32[6,3,2,8,128]{4,3,2,1,0:T(8,128)} %b_hbm.1, s32[2,8,128]{2,1,0:T(8,128)} %d_hbm.1, s32[2,8,128]{2,1,0:T(8,128)} %s_hbm.1), custom_call_target="tpu_custom_call" | custom-call | tf_op jit(solution)/shard_map/pallas_call | solution.py:757
  74.8 0.0 copy-done
  74.8 1.7 %fusion = (f32[6,3,2,8,128]{4,3,2,1,0:T(8,128)}, f32[6,3,2,8,128]{4,3,2,1,0:T(8,128)}) fusion(f32[6,3,2,8,128]{4,3,2,1,0:T(8,128)} %get-tuple-element.5, f32[6,3,2,8,128]{4,3,2,1,0:T(8,128)S(1)} %copy-done, f32[6,3,2,8,128]{4,3,2,1,0:T(8,128)} %get-tuple-element.4), kind=kLoop, calls=%fused_computation | loop fusion | flops 73728 | bytes 737280 | tf_op jit(solution)/shard_map/sub | solution.py:766
Async XLA Ops:
  0.6 74.2 %copy-start = (f32[6,3,2,8,128]{4,3,2,1,0:T(8,128)S(1)}, f32[6,3,2,8,128]{4,3,2,1,0:T(8,128)}, u32[]{:S(2)}) copy-start(f32[6,3,2,8,128]{4,3,2,1,0:T(8,128)} %x_hbm.1) | copy-start | bytes 442372

commit v4 on v3

--- a/solution.py
+++ b/solution.py
@@ -220,34 +220,62 @@
             if conds:
                 exists[dx, dy] = functools.reduce(jnp.logical_and, conds)
 
-    greet(gx, gy, oz)
-    expected = 1
-    for (dx, dy), here in exists.items():
-
+    def greet_if(here, targets):
         @pl.when(here)
-        def _(dx=dx, dy=dy):
-            for core in (0, 1):
-                greet(gx + dx, gy + dy, core)
-
-        expected = expected + 2 * here.astype(jnp.int32)
-
-    def round_of(number):
-        step = 2**number
-        for size, mine, place in ((nx, gx, lambda c: (c, gy)), (ny, gy, lambda c: (gx, c))):
-            if step < size:
-                for d in (step, -step):
-                    yield (mine + d < size if d > 0 else mine + d >= 0), place(mine + d)
-
-    def tell(number):
-        for here, (cx, cy) in round_of(number):
-
-            @pl.when(here)
-            def _(cx=cx, cy=cy):
-                pl.semaphore_signal(heard.at[number], inc=1, device_id=(grp, cx, cy, gz), device_id_type=MESH)
-
-    def hear(number):
-        count = sum(here.astype(jnp.int32) for here, _ in round_of(number))
-        pl.semaphore_wait(heard.at[number], count)
+        def _():
+            for target in targets:
+                greet(*target)
+
+    bottom = gx == 0
+    expected = bottom.astype(jnp.int32)
+    for dy in (-1, 0, 1):
+        greet_if(exists[1, dy], [(gx + 1, gy + dy, core) for core in (0, 1)])
+        expected = expected + 2 * exists[-1, dy].astype(jnp.int32)
+        if dy:
+            here = jnp.logical_and(bottom, exists[0, dy])
+            greet_if(here, [(gx, gy + dy, core) for core in (0, 1)])
+            expected = expected + 2 * here.astype(jnp.int32)
+        else:
+            greet_if(bottom, [(gx, gy, oz)])
+
+    def signal(index, cx, cy, cz):
+        pl.semaphore_signal(heard.at[index], inc=1, device_id=(grp, cx, cy, cz), device_id_type=MESH)
+
+    def signal_if(here, index, cx, cy, cz):
+        pl.when(here)(lambda: signal(index, cx, cy, cz))
+
+    def count_of(*conds):
+        return sum(c.astype(jnp.int32) for c in conds)
+
+    def wait_heard(index, each, *conds):
+        @pl.when(functools.reduce(jnp.logical_or, conds))
+        def _():
+            pl.semaphore_wait(heard.at[index], each * count_of(*conds))
+
+    def tell_y(k):
+        step = 2**k
+        if step < ny:
+            signal_if(gy + step < ny, 1 + k, gx, gy + step, gz)
+            signal_if(gy >= step, 1 + k, gx, gy - step, gz)
+
+    def hear_y(k):
+        step = 2**k
+        if step < ny:
+            wait_heard(1 + k, 1, gy + step < ny, gy >= step)
+
+    def tell_x(k):
+        step = 2**k
+        if step < nx:
+            signal_if(gx + step < nx, 4 + k, gx + step, gy, gz)
+            signal_if(gx >= step, 8 + k, gx - step, gy, gz)
+
+    def hear_x(k, below=True, above=True):
+        step = 2**k
+        if step < nx:
+            if below:
+                wait_heard(4 + k, 1, gx >= step)
+            if above:
+                wait_heard(8 + k, 1, gx + step < nx)
 
     def clear(ref, *index):
         ref[index] = jnp.zeros(ref[index].shape, f32)
@@ -284,6 +312,15 @@
         clear(yrow, pl.ds(4, 4))
         for u in (u1, u2):
             clear(u, full, full, 9)
+
+    mark('barrier')
+    pl.semaphore_wait(barrier, expected)
+    for dy in (0, -1, 1):
+
+        @pl.when(exists[-1, dy])
+        def _(dy=dy):
+            for core in (0, 1):
+                signal(0, gx - 1, gy + dy, core)
 
     mark('prep')
     loads[0].wait()
@@ -312,9 +349,6 @@
                 for side, y in ((0, 0), (1, 7)):
                     ysend[side, core, p, 4 * k + comp:4 * k + comp + 1] = t[y:y + 1]
 
-    mark('barrier')
-    pl.semaphore_wait(barrier, expected)
-    tell(0)
     mark('send1')
 
     def view(ref, *index):
@@ -357,7 +391,8 @@
     half_16 = pl.ds(pl.multiple_of(16 * gz, 8), 16)
     other_rows = pl.ds(pl.multiple_of(32 * oz, 8), 24)
     bytes1 = {}
-    for key in sorted(exists, key=lambda k: (k[1] == 0, -abs(k[0]))):
+
+    def send_start(key):
         dx, dy = key
         items, count = [], 0
         p, there_p = (1, 0) if dx > 0 else (0, 3)
@@ -384,11 +419,11 @@
                     count += 8
         exchange(exists[key], slot[key], slot[key], items)
         bytes1[key] = count
-    exchange(None, 8, 16, [
-        (view(xm, oz), view(nat, pl.ds(3, 6), half_rows), partner),
-        (view(esend), view(enat, gz, pl.ds(1, 4)), partner),
-    ])
-
+
+    order = sorted(exists, key=lambda k: (k[1] == 0, -abs(k[0])))
+    for key in order:
+        if key[0] < 0:
+            send_start(key)
     mark('points')
     for load in loads[3:]:
         load.wait()
@@ -417,19 +452,35 @@
             for comp in range(3):
                 total = bin_[case, comp, p] + points[(case * 2 + p) * 3 + comp]
                 qs[core, p * 3 + comp, 8 * k:8 * k + 8] = m * total - (1.0 - m) * xin[case, comp, p]
-    exchange(None, 9, 17, [(view(qs, oz), view(qnat, full, half_rows), partner)])
     for k in range(6):
         nat[3 + k, half_rows] = xm[gz, k]
         qnat[k, half_rows] = qs[gz, k]
 
-    hear(0)
-    tell(1)
+    mark('above')
+    wait_heard(0, 2, *(exists[1, dy] for dy in (-1, 0, 1)))
+    signal_if(gx < nx - 1, 12, gx + 1, gy, gz)
+    for key in order:
+        if key[0] > 0:
+            send_start(key)
+    wait_heard(12, 1, gx > 0)
+    for key in order:
+        if key[0] == 0:
+            send_start(key)
+    exchange(None, 8, 16, [
+        (view(xm, oz), view(nat, pl.ds(3, 6), half_rows), partner),
+        (view(esend), view(enat, gz, pl.ds(1, 4)), partner),
+    ])
+    exchange(None, 9, 17, [(view(qs, oz), view(qnat, full, half_rows), partner)])
+    tell_x(0)
+    tell_y(0)
     mark('wait1')
     for (dx, dy), index in slot.items():
         wait_in(exists[-dx, -dy], index, rows_of(bytes1[dx, dy]))
     wait_in(None, 16, rows_of(176))
-    hear(1)
-    tell(2)
+    hear_x(0)
+    tell_x(1)
+    hear_y(0)
+    tell_y(1)
     mark('build')
 
     low = sub < 4
@@ -533,8 +584,6 @@
     share(rb, 8, 18)
     mark('wait2')
     take_halos(u1, 8)
-    hear(2)
-    tell(3)
     mark('k2')
 
     def second(y, force):
@@ -553,6 +602,10 @@
     wait_out(None, 9, view(qs, oz))
     swap_halos(u2, 0)
     share(ib, 9, 19)
+    hear_x(1)
+    tell_x(2)
+    hear_y(1)
+    tell_y(2)
     wait_in(None, 18, view(rb, oz))
     wait_in(None, 19, view(ib, oz))
 
@@ -617,6 +670,7 @@
         jnp.ones((8, 128), f32), ga[...], (((1,), (1,)), ((), ())),
         precision=lax.Precision.HIGHEST, preferred_element_type=f32,
     )
+    hear_y(2)
     mark('reduce_a')
     me = gz * ny + gy
     ag[me] = row[0:1]
@@ -624,17 +678,23 @@
         (view(ag, me), view(ag, me), (grp, gx, lax.rem(gy + d, ny), oz if flip else gz))
         for d in range(ny) for flip in (0, 1) if d or flip
     ])
+    hear_x(2)
+    tell_x(3)
     wait_in(None, 21, view(ag, pl.ds(0, 2 * ny - 1)))
     for s in (0, 1):
         total = ag[s * ny]
         for k in range(1, ny):
             total = total + ag[s * ny + k]
         bg[gx, s:s + 1] = total
-    hear(3)
+    hear_x(3, above=False)
     mark('reduce_b')
-    exchange(None, 11, 22, [
-        (view(bg, gx), view(bg, gx), (grp, lax.rem(gx + d, nx), gy, gz)) for d in range(1, nx)
-    ])
+    def send_sum(target, carry):
+        descriptor(view(bg, gx), view(bg, gx), 11, 22, (grp, target, gy, gz)).start()
+        return carry
+
+    lax.fori_loop(0, gx, send_sum, 0)
+    hear_x(3, below=False)
+    lax.fori_loop(gx + 1, nx, send_sum, 0)
     wait_in(None, 22, view(bg, pl.ds(0, nx - 1)))
     mark('solve')
     total = bg[0]
@@ -751,7 +811,7 @@
         vmem(128, 128), vmem(2 * ny, 1, 128), vmem(nx, 2, 128), vmem(176, 128), vmem(*block), vmem(*block),
         pltpu.SMEM(load_nodes.shape, jnp.int32), pltpu.SMEM((CASES, 3, LOADS), f32),
         pltpu.SemaphoreType.DMA((6,)), pltpu.SemaphoreType.DMA((2,)), pltpu.SemaphoreType.DMA((12,)), pltpu.SemaphoreType.DMA((23,)),
-        pltpu.SemaphoreType.REGULAR((4,)),
+        pltpu.SemaphoreType.REGULAR((13,)),
     ]
     out = jax.ShapeDtypeStruct(block, f32)
     change, shifted = pl.pallas_call(

time: 76.7 us -> 75.1 us (0.979)
  Pallas kernels: 74.2 us -> 72.5 us
    pallas_call x1, Pallas kernels: 74.2 us -> 72.5 us  [shards(): pl.pallas_call(functools.partial(kernel, nx, ny), out_shape=(out, out), i...]
where the time goes in v4:
time: 75.1 us; the launch traced here: 74.9 us
  Pallas kernels  72.5 us (97%)
  other arithmetic  1.72 us (2%)
    pallas_call x1, Pallas kernels, shards(): pl.pallas_call(functools.partial(kernel, nx, ny), out_shape=(out, out), i...  72.5 us
    sub x1, other arithmetic, shards(): return (start + change, shifted - start)  1.72 us

profile of v4, /device:TPU:65, one launch (start us, length us, event | category | flops | bytes accessed | tf_op | source)
XLA Modules:
  0.0 74.9 jit_solution(17176263968121644127)
XLA Ops:
  0.6 0.0 copy-start
  0.6 72.5 %shard_map.77 = (f32[6,3,2,8,128]{4,3,2,1,0:T(8,128)}, f32[6,3,2,8,128]{4,3,2,1,0:T(8,128)}) custom-call(s32[6,16]{1,0:T(8,128)} %n_hbm.1, f32[6,3,16]{2,1,0:T(4,128)} %bitcast.1, f32[6,3,2,8,128]{4,3,2,1,0:T(8,128)} %x_hbm.1, f32[6,3,2,8,128]{4,3,2,1,0:T(8,128)} %b_hbm.1, s32[2,8,128]{2,1,0:T(8,128)} %d_hbm.1, s32[2,8,128]{2,1,0:T(8,128)} %s_hbm.1), custom_call_target="tpu_custom_call" | custom-call | tf_op jit(solution)/shard_map/pallas_call | solution.py:817
  73.2 0.0 copy-done
  73.2 1.7 %fusion = (f32[6,3,2,8,128]{4,3,2,1,0:T(8,128)}, f32[6,3,2,8,128]{4,3,2,1,0:T(8,128)}) fusion(f32[6,3,2,8,128]{4,3,2,1,0:T(8,128)} %get-tuple-element.5, f32[6,3,2,8,128]{4,3,2,1,0:T(8,128)S(1)} %copy-done, f32[6,3,2,8,128]{4,3,2,1,0:T(8,128)} %get-tuple-element.4), kind=kLoop, calls=%fused_computation | loop fusion | flops 73728 | bytes 737280 | tf_op jit(solution)/shard_map/sub | solution.py:826
Async XLA Ops:
  0.6 72.5 %copy-start = (f32[6,3,2,8,128]{4,3,2,1,0:T(8,128)S(1)}, f32[6,3,2,8,128]{4,3,2,1,0:T(8,128)}, u32[]{:S(2)}) copy-start(f32[6,3,2,8,128]{4,3,2,1,0:T(8,128)} %x_hbm.1) | copy-start | bytes 442372

commit v5 on v4

--- a/solution.py
+++ b/solution.py
@@ -75,25 +75,33 @@
     return g
 
 
-def apply_k(node_row, em_row, emit, lane, sub):
-    prev_z = None
-    prev_hi = None
-    for r in range(10):
-        zs = []
-        for c in range(3):
-            v = node_row(c, r)
-            w = z_up(v, lane, sub)
-            zs.append((v + w, w - v))
-        if r > 0:
+class Stiffness:
+    def __init__(self, node_row, em_row, emit, lane, sub):
+        self.node_row, self.em_row, self.emit, self.lane, self.sub = node_row, em_row, emit, lane, sub
+        self.nodes, self.elements = {}, {}
+
+    def node(self, r):
+        if r not in self.nodes:
+            zs = []
+            for c in range(3):
+                v = self.node_row(c, r)
+                w = z_up(v, self.lane, self.sub)
+                zs.append((v + w, w - v))
+            self.nodes[r] = zs
+        return self.nodes[r]
+
+    def element(self, j):
+        if j not in self.elements:
+            low_row, high_row = self.node(j), self.node(j + 1)
             a = {}
             for c in range(3):
                 for z in (0, 1):
-                    lo, hi = prev_z[c][z], zs[c][z]
+                    lo, hi = low_row[c][z], high_row[c][z]
                     for y, f in ((0, lo + hi), (1, hi - lo)):
                         a[c, 1, y, z] = f[1:4] - f[0:3]
                         if y or z:
                             a[c, 0, y, z] = f[0:3] + f[1:4]
-            g = modal(a, em_row(r - 1))
+            g = modal(a, self.em_row(j))
             lows, highs = [], []
             for c in range(3):
                 h = {}
@@ -107,15 +115,18 @@
                         h[y, z] = t
                 lows.append([h[0, z] - h[1, z] for z in (0, 1)])
                 highs.append([h[0, z] + h[1, z] for z in (0, 1)])
-            if r > 1:
-                out = []
-                for c in range(3):
-                    ks = prev_hi[c][0] + lows[c][0]
-                    kd = prev_hi[c][1] + lows[c][1]
-                    out.append((ks - kd) + z_dn(ks + kd, lane, sub))
-                emit(r - 2, out)
-            prev_hi = highs
-        prev_z = zs
+            self.elements[j] = lows, highs
+        return self.elements[j]
+
+    def rows(self, *ys):
+        for y in ys:
+            highs, lows = self.element(y)[1], self.element(y + 1)[0]
+            out = []
+            for c in range(3):
+                ks = highs[c][0] + lows[c][0]
+                kd = highs[c][1] + lows[c][1]
+                out.append((ks - kd) + z_dn(ks + kd, self.lane, self.sub))
+            self.emit(y, out)
 
 
 def cyc1(v, sub):
@@ -320,7 +331,7 @@
         @pl.when(exists[-1, dy])
         def _(dy=dy):
             for core in (0, 1):
-                signal(0, gx - 1, gy + dy, core)
+                signal(13 if dy else 0, gx - 1, gy + dy, core)
 
     mark('prep')
     loads[0].wait()
@@ -457,11 +468,12 @@
         qnat[k, half_rows] = qs[gz, k]
 
     mark('above')
-    wait_heard(0, 2, *(exists[1, dy] for dy in (-1, 0, 1)))
+    wait_heard(0, 2, exists[1, 0])
+    send_start((1, 0))
+    wait_heard(13, 2, exists[1, -1], exists[1, 1])
     signal_if(gx < nx - 1, 12, gx + 1, gy, gz)
-    for key in order:
-        if key[0] > 0:
-            send_start(key)
+    send_start((1, -1))
+    send_start((1, 1))
     wait_heard(12, 1, gx > 0)
     for key in order:
         if key[0] == 0:
@@ -519,6 +531,66 @@
     def at(y):
         return pl.ds(8 * y, 8)
 
+    def halo_views(u, key, chunk):
+        dx, dy = key
+        src, dst = (2, 0) if dx > 0 else (1, 3)
+        ysrc, ydst = (8, 0) if dy > 0 else (1, 9)
+        if dy == 0:
+            return [
+                (view(u, full, src, pl.ds(k, m)), view(u, full, dst, pl.ds(k, m)))
+                for k, m in (((1, 2), (7, 1)) if chunk == 0 else ((3, 3),))
+            ]
+        if dx == 0:
+            return [(view(u, full, pl.ds(1, 2), ysrc), view(u, full, pl.ds(1, 2), ydst))]
+        return [(view(u, full, src, ysrc), view(u, full, dst, ydst))]
+
+    halo_rows = {(dx, dy): 8 * 3 * (6 if dy == 0 else 2 if dx == 0 else 1) for dx, dy in exists}
+
+    free = sub % 4 == 3
+    chunks = ((1, 2, 7, 8), (3, 4, 5, 6))
+
+    def pack(u, chunk):
+        *carriers, last = chunks[chunk]
+        t = u[:, 1:3, last]
+        for i, k in enumerate(carriers, 1):
+            u[:, 1:3, k] = jnp.where(free, pltpu.roll(t, 4 - i, axis=2), u[:, 1:3, k])
+
+    def unpack(u, chunk):
+        *carriers, last = chunks[chunk]
+        for p in (0, 3):
+            a, b, c = (pltpu.roll(u[:, p, k], 4 + i, axis=1) for i, k in enumerate(carriers, 1))
+            u[:, p, last] = jnp.where(sub % 4 == 0, a, jnp.where(sub % 4 == 1, b, c))
+
+    def halo_slot(first_slot, key, chunk):
+        if chunk == 0:
+            return first_slot + slot[key]
+        return 23 + 2 * (first_slot == 0) + (key[0] > 0)
+
+    def send_halos(u, first_slot, chunk):
+        pack(u, chunk)
+        for key in order:
+            dx, dy = key
+            if chunk == 0 or dy == 0:
+                exchange(
+                    exists[key], slot[key], halo_slot(first_slot, key, chunk),
+                    [(a, b, (grp, gx + dx, gy + dy, gz)) for a, b in halo_views(u, key, chunk)],
+                )
+
+    def take_halos(u, first_slot, chunk):
+        for key in exists:
+            dx, dy = key
+            if chunk == 0 or dy == 0:
+                rows = halo_rows[key] // 2 if dy == 0 else halo_rows[key]
+                wait_in(exists[-dx, -dy], halo_slot(first_slot, key, chunk), rows_of(rows))
+        unpack(u, chunk)
+
+    def sent_halos(u):
+        for key in exists:
+            wait_out(exists[key], slot[key], rows_of(halo_rows[key]))
+
+    def share(buf, send_index, recv_index):
+        exchange(None, send_index, recv_index, [(view(buf, gz), view(buf, gz), partner)])
+
     def first(y, force):
         m = mob[:, at(y)]
         s = scl[:, at(y)]
@@ -528,62 +600,20 @@
             rb[gz, comp, :, at(y)] = res
             u1[comp, 1:3, 1 + y] = m * (s * res)
 
-    apply_k(lambda c, r: u0[c, :, r], lambda j: em[j], first, lane, sub)
-
-    def halo_views(u, key):
-        dx, dy = key
-        src, dst = (2, 0) if dx > 0 else (1, 3)
-        ysrc, ydst = (8, 0) if dy > 0 else (1, 9)
-        if dy == 0:
-            return [(view(u, full, src, pl.ds(k, 3)), view(u, full, dst, pl.ds(k, 3))) for k in (1, 5)]
-        if dx == 0:
-            return [(view(u, full, pl.ds(1, 2), ysrc), view(u, full, pl.ds(1, 2), ydst))]
-        return [(view(u, full, src, ysrc), view(u, full, dst, ydst))]
-
-    halo_rows = {(dx, dy): 8 * 3 * (6 if dy == 0 else 2 if dx == 0 else 1) for dx, dy in exists}
-
-    free = sub % 4 == 3
-
-    def pack(u):
-        for k in (0, 4):
-            t = u[:, 1:3, k + 4]
-            for i in (1, 2, 3):
-                u[:, 1:3, k + i] = jnp.where(free, pltpu.roll(t, 4 - i, axis=2), u[:, 1:3, k + i])
-
-    def unpack(u):
-        for p in (0, 3):
-            for k in (0, 4):
-                a, b, c = (pltpu.roll(u[:, p, k + i], 4 + i, axis=1) for i in (1, 2, 3))
-                u[:, p, k + 4] = jnp.where(sub % 4 == 0, a, jnp.where(sub % 4 == 1, b, c))
-
-    def swap_halos(u, first_slot):
-        pack(u)
-        for key in sorted(exists, key=lambda k: (k[1] == 0, -abs(k[0]))):
-            dx, dy = key
-            exchange(
-                exists[key], slot[key], first_slot + slot[key],
-                [(a, b, (grp, gx + dx, gy + dy, gz)) for a, b in halo_views(u, key)],
-            )
-
-    def take_halos(u, first_slot):
-        for dx, dy in exists:
-            wait_in(exists[-dx, -dy], first_slot + slot[dx, dy], rows_of(halo_rows[dx, dy]))
-        unpack(u)
-
-    def sent_halos(u):
-        for key in exists:
-            wait_out(exists[key], slot[key], rows_of(halo_rows[key]))
-
-    def share(buf, send_index, recv_index):
-        exchange(None, send_index, recv_index, [(view(buf, gz), view(buf, gz), partner)])
-
+    def em_row(j):
+        return em[j]
+
+    stiff = Stiffness(lambda c, r: u0[c, :, r], em_row, first, lane, sub)
+    stiff.rows(0, 7, 1, 6)
     for key in exists:
         wait_out(exists[key], slot[key], rows_of(bytes1[key]))
     wait_out(None, 8, rows_of(176))
-    swap_halos(u1, 8)
+    send_halos(u1, 8, 0)
+    stiff.rows(2, 3, 4, 5)
+    send_halos(u1, 8, 1)
     share(rb, 8, 18)
     mark('wait2')
-    take_halos(u1, 8)
+    take_halos(u1, 8, 0)
     mark('k2')
 
     def second(y, force):
@@ -595,12 +625,16 @@
             ib[gz, comp, :, at(y)] = image
             u2[comp, 1:3, 1 + y] = m * (s * image)
 
-    apply_k(lambda c, r: u1[c, :, r], lambda j: em[j], second, lane, sub)
-
+    stiff = Stiffness(lambda c, r: u1[c, :, r], em_row, second, lane, sub)
+    stiff.rows(0, 7)
+    take_halos(u1, 8, 1)
+    stiff.rows(1, 6)
+    sent_halos(u1)
+    send_halos(u2, 0, 0)
+    stiff.rows(2, 3, 4, 5)
+    send_halos(u2, 0, 1)
     mark('send3')
-    sent_halos(u1)
     wait_out(None, 9, view(qs, oz))
-    swap_halos(u2, 0)
     share(ib, 9, 19)
     hear_x(1)
     tell_x(2)
@@ -637,7 +671,7 @@
     sums = grams(make_g) + grams(make_h) + grams(make_p)
 
     mark('wait3')
-    take_halos(u2, 0)
+    take_halos(u2, 0, 0)
     mark('k3')
 
     jacc = []
@@ -656,7 +690,10 @@
             else:
                 jacc.append(prods)
 
-    apply_k(lambda c, r: u2[c, :, r], lambda j: em[j], third, lane, sub)
+    stiff = Stiffness(lambda c, r: u2[c, :, r], em_row, third, lane, sub)
+    stiff.rows(0, 7)
+    take_halos(u2, 0, 1)
+    stiff.rows(1, 6, 2, 3, 4, 5)
     wait_out(None, 8, view(rb, gz))
     share(yb, 8, 20)
     sums = sums + [a[0] + a[1] for a in jacc[0]]
@@ -676,7 +713,7 @@
     ag[me] = row[0:1]
     exchange(None, 10, 21, [
         (view(ag, me), view(ag, me), (grp, gx, lax.rem(gy + d, ny), oz if flip else gz))
-        for d in range(ny) for flip in (0, 1) if d or flip
+        for d in sorted(range(ny), key=lambda d: -min(d, ny - d)) for flip in (0, 1) if d or flip
     ])
     hear_x(2)
     tell_x(3)
@@ -810,8 +847,8 @@
         vmem(2, 3, 2, 64, 128), vmem(2, 3, 2, 64, 128), vmem(2, 3, 2, 64, 128),
         vmem(128, 128), vmem(2 * ny, 1, 128), vmem(nx, 2, 128), vmem(176, 128), vmem(*block), vmem(*block),
         pltpu.SMEM(load_nodes.shape, jnp.int32), pltpu.SMEM((CASES, 3, LOADS), f32),
-        pltpu.SemaphoreType.DMA((6,)), pltpu.SemaphoreType.DMA((2,)), pltpu.SemaphoreType.DMA((12,)), pltpu.SemaphoreType.DMA((23,)),
-        pltpu.SemaphoreType.REGULAR((13,)),
+        pltpu.SemaphoreType.DMA((6,)), pltpu.SemaphoreType.DMA((2,)), pltpu.SemaphoreType.DMA((12,)), pltpu.SemaphoreType.DMA((27,)),
+        pltpu.SemaphoreType.REGULAR((14,)),
     ]
     out = jax.ShapeDtypeStruct(block, f32)
     change, shifted = pl.pallas_call(

time: 75.1 us -> 74.9 us (level)
  no operation moved by 1% of the time
where the time goes in v5:
time: 74.9 us; the launch traced here: 74.7 us
  Pallas kernels  72.3 us (97%)
  other arithmetic  1.72 us (2%)
    pallas_call x1, Pallas kernels, shards(): pl.pallas_call(functools.partial(kernel, nx, ny), out_shape=(out, out), i...  72.3 us
    sub x1, other arithmetic, shards(): return (start + change, shifted - start)  1.72 us

profile of v5, /device:TPU:65, one launch (start us, length us, event | category | flops | bytes accessed | tf_op | source)
XLA Modules:
  0.0 74.7 jit_solution(5647225674331681246)
XLA Ops:
  0.6 0.0 copy-start
  0.6 72.3 %shard_map.77 = (f32[6,3,2,8,128]{4,3,2,1,0:T(8,128)}, f32[6,3,2,8,128]{4,3,2,1,0:T(8,128)}) custom-call(s32[6,16]{1,0:T(8,128)} %n_hbm.1, f32[6,3,16]{2,1,0:T(4,128)} %bitcast.1, f32[6,3,2,8,128]{4,3,2,1,0:T(8,128)} %x_hbm.1, f32[6,3,2,8,128]{4,3,2,1,0:T(8,128)} %b_hbm.1, s32[2,8,128]{2,1,0:T(8,128)} %d_hbm.1, s32[2,8,128]{2,1,0:T(8,128)} %s_hbm.1), custom_call_target="tpu_custom_call" | custom-call | tf_op jit(solution)/shard_map/pallas_call | solution.py:854
  73.0 0.0 copy-done
  73.0 1.7 %fusion = (f32[6,3,2,8,128]{4,3,2,1,0:T(8,128)}, f32[6,3,2,8,128]{4,3,2,1,0:T(8,128)}) fusion(f32[6,3,2,8,128]{4,3,2,1,0:T(8,128)} %get-tuple-element.5, f32[6,3,2,8,128]{4,3,2,1,0:T(8,128)S(1)} %copy-done, f32[6,3,2,8,128]{4,3,2,1,0:T(8,128)} %get-tuple-element.4), kind=kLoop, calls=%fused_computation | loop fusion | flops 73728 | bytes 737280 | tf_op jit(solution)/shard_map/sub | solution.py:863
Async XLA Ops:
  0.6 72.3 %copy-start = (f32[6,3,2,8,128]{4,3,2,1,0:T(8,128)S(1)}, f32[6,3,2,8,128]{4,3,2,1,0:T(8,128)}, u32[]{:S(2)}) copy-start(f32[6,3,2,8,128]{4,3,2,1,0:T(8,128)} %x_hbm.1) | copy-start | bytes 442372

commit v6 on v5

--- a/solution.py
+++ b/solution.py
@@ -154,7 +154,7 @@
         s = m[j, j]
         for k in range(j):
             s = s - low[j, k] * low[j, k]
-        inv[j] = 1.0 / jnp.sqrt(s)
+        inv[j] = lax.rsqrt(s)
         for i in range(j + 1, n):
             t = m[i, j]
             for k in range(j):
@@ -188,7 +188,7 @@
     n_hbm, v_hbm, x_hbm, b_hbm, d_hbm, s_hbm,
     xo_hbm, ro_hbm,
     xin, bin_, din, sin, xm, ysend, esend, qs,
-    nat, yrow, enat, ey, qnat,
+    nat, yrow, enat, qnat,
     u0, u1, u2, em, mob, scl, rb, ib, yb, ga, ag, bg, dummy, xout, rout, nodes, vals,
     in_sem, out_sem, ss, rs, heard,
 ):
@@ -297,7 +297,6 @@
     def _():
         clear(nat, pl.ds(0, 3))
         clear(enat, full, 0)
-        clear(ey, full, 0)
         for side in (0, 4):
             clear(yrow, side)
         for u in (u1, u2):
@@ -314,7 +313,6 @@
     @pl.when(gy == 0)
     def _():
         clear(yrow, pl.ds(0, 4))
-        clear(ey)
         for u in (u1, u2):
             clear(u, full, full, 0)
 
@@ -351,6 +349,8 @@
         for core in range(2):
             for p in range(2):
                 ysend[side, core, p, 8:16] = jnp.zeros((8, 128), f32)
+                if side == 1:
+                    ysend[side, core, p, 12:13] = esend[p, 7:8]
     for case in range(CASES):
         core, k = divmod(case, HALF)
         for comp in range(3):
@@ -419,15 +419,9 @@
             elif dx == 0:
                 items.append((view(ysend, side, core), view(yrow, pl.ds(4 * there + 1, 2), half_16), device))
                 count += 32
-                if dy > 0:
-                    items.append((view(esend, pl.ds(0, 2)), view(ey, gz, pl.ds(1, 2)), device))
-                    count += 16
             else:
                 items.append((view(ysend, side, core, p), view(yrow, 4 * there + there_p, half_16), device))
                 count += 16
-                if dx > 0 and dy > 0:
-                    items.append((view(esend, pl.ds(1, 1)), view(ey, gz, pl.ds(0, 1)), device))
-                    count += 8
         exchange(exists[key], slot[key], slot[key], items)
         bytes1[key] = count
 
@@ -502,7 +496,10 @@
 
     for j in range(9):
         for e in range(3):
-            t = spread(ey, e, 7) if j == 0 else spread(enat, e, j - 1)
+            if j == 0:
+                t = jnp.where(low, yrow[e, 12:13], yrow[e, 28:29])
+            else:
+                t = spread(enat, e, j - 1)
             em[j, e] = t * (MU / 16.0)
     for y in range(8):
         rows = em[y] + em[y + 1]
@@ -614,6 +611,7 @@
     share(rb, 8, 18)
     mark('wait2')
     take_halos(u1, 8, 0)
+    take_halos(u1, 8, 1)
     mark('k2')
 
     def second(y, force):
@@ -627,7 +625,6 @@
 
     stiff = Stiffness(lambda c, r: u1[c, :, r], em_row, second, lane, sub)
     stiff.rows(0, 7)
-    take_halos(u1, 8, 1)
     stiff.rows(1, 6)
     sent_halos(u1)
     send_halos(u2, 0, 0)
@@ -841,7 +838,7 @@
     scratch = [
         vmem(*block), vmem(*block), pltpu.VMEM(design.shape, jnp.int32), pltpu.VMEM(design.shape, jnp.int32),
         vmem(2, 6, 24, 128), vmem(2, 2, 2, 16, 128), vmem(4, 8, 128), vmem(2, 6, 24, 128),
-        vmem(12, 64, 128), vmem(8, 32, 128), vmem(2, 5, 8, 128), vmem(2, 3, 8, 128), vmem(6, 64, 128),
+        vmem(12, 64, 128), vmem(8, 32, 128), vmem(2, 5, 8, 128), vmem(6, 64, 128),
         vmem(3, 4, 10, 8, 128), vmem(3, 4, 10, 8, 128), vmem(3, 4, 10, 8, 128),
         vmem(9, 3, 8, 128), vmem(2, 64, 128), vmem(2, 64, 128),
         vmem(2, 3, 2, 64, 128), vmem(2, 3, 2, 64, 128), vmem(2, 3, 2, 64, 128),

time: 74.9 us -> 74.5 us (level)
  no operation moved by 1% of the time
where the time goes in v6:
time: 74.5 us; the launch traced here: 74.3 us
  Pallas kernels  71.9 us (97%)
  other arithmetic  1.72 us (2%)
    pallas_call x1, Pallas kernels, shards(): pl.pallas_call(functools.partial(kernel, nx, ny), out_shape=(out, out), i...  71.9 us
    sub x1, other arithmetic, shards(): return (start + change, shifted - start)  1.72 us

profile of v6, /device:TPU:65, one launch (start us, length us, event | category | flops | bytes accessed | tf_op | source)
XLA Modules:
  0.0 74.3 jit_solution(7026532890907456436)
XLA Ops:
  0.6 0.0 copy-start
  0.6 71.9 %shard_map.77 = (f32[6,3,2,8,128]{4,3,2,1,0:T(8,128)}, f32[6,3,2,8,128]{4,3,2,1,0:T(8,128)}) custom-call(s32[6,16]{1,0:T(8,128)} %n_hbm.1, f32[6,3,16]{2,1,0:T(4,128)} %bitcast.1, f32[6,3,2,8,128]{4,3,2,1,0:T(8,128)} %x_hbm.1, f32[6,3,2,8,128]{4,3,2,1,0:T(8,128)} %b_hbm.1, s32[2,8,128]{2,1,0:T(8,128)} %d_hbm.1, s32[2,8,128]{2,1,0:T(8,128)} %s_hbm.1), custom_call_target="tpu_custom_call" | custom-call | tf_op jit(solution)/shard_map/pallas_call | solution.py:851
  72.6 0.0 copy-done
  72.6 1.7 %fusion = (f32[6,3,2,8,128]{4,3,2,1,0:T(8,128)}, f32[6,3,2,8,128]{4,3,2,1,0:T(8,128)}) fusion(f32[6,3,2,8,128]{4,3,2,1,0:T(8,128)} %get-tuple-element.5, f32[6,3,2,8,128]{4,3,2,1,0:T(8,128)S(1)} %copy-done, f32[6,3,2,8,128]{4,3,2,1,0:T(8,128)} %get-tuple-element.4), kind=kLoop, calls=%fused_computation | loop fusion | flops 73728 | bytes 737280 | tf_op jit(solution)/shard_map/sub | solution.py:860
Async XLA Ops:
  0.6 71.9 %copy-start = (f32[6,3,2,8,128]{4,3,2,1,0:T(8,128)S(1)}, f32[6,3,2,8,128]{4,3,2,1,0:T(8,128)}, u32[]{:S(2)}) copy-start(f32[6,3,2,8,128]{4,3,2,1,0:T(8,128)} %x_hbm.1) | copy-start | bytes 442372

commit v7 on v6

--- a/solution.py
+++ b/solution.py
@@ -76,45 +76,74 @@
 
 
 class Stiffness:
-    def __init__(self, node_row, em_row, emit, lane, sub):
-        self.node_row, self.em_row, self.emit, self.lane, self.sub = node_row, em_row, emit, lane, sub
-        self.nodes, self.elements = {}, {}
-
-    def node(self, r):
-        if r not in self.nodes:
+    def __init__(self, planes, em_at, emit, lane, sub):
+        self.planes, self.em_at, self.emit, self.lane, self.sub = planes, em_at, emit, lane, sub
+        self.nodes, self.fields_, self.middles, self.elements = {}, {}, {}, {}
+
+    def node(self, r, which):
+        if (r, which) not in self.nodes:
             zs = []
             for c in range(3):
-                v = self.node_row(c, r)
+                v = self.planes(c, r, which)
                 w = z_up(v, self.lane, self.sub)
                 zs.append((v + w, w - v))
-            self.nodes[r] = zs
-        return self.nodes[r]
-
-    def element(self, j):
-        if j not in self.elements:
-            low_row, high_row = self.node(j), self.node(j + 1)
-            a = {}
+            self.nodes[r, which] = zs
+        return self.nodes[r, which]
+
+    def fields(self, j, which):
+        if (j, which) not in self.fields_:
+            low_row, high_row = self.node(j, which), self.node(j + 1, which)
+            f = {}
             for c in range(3):
                 for z in (0, 1):
                     lo, hi = low_row[c][z], high_row[c][z]
-                    for y, f in ((0, lo + hi), (1, hi - lo)):
-                        a[c, 1, y, z] = f[1:4] - f[0:3]
-                        if y or z:
-                            a[c, 0, y, z] = f[0:3] + f[1:4]
-            g = modal(a, self.em_row(j))
-            lows, highs = [], []
-            for c in range(3):
-                h = {}
-                for y in (0, 1):
-                    for z in (0, 1):
-                        gd = g[c, 1, y, z]
-                        t = gd[0:2] - gd[1:3]
-                        if y or z:
-                            gs = g[c, 0, y, z]
-                            t = t + (gs[0:2] + gs[1:3])
-                        h[y, z] = t
-                lows.append([h[0, z] - h[1, z] for z in (0, 1)])
-                highs.append([h[0, z] + h[1, z] for z in (0, 1)])
+                    f[c, 0, z], f[c, 1, z] = lo + hi, hi - lo
+            self.fields_[j, which] = f
+        return self.fields_[j, which]
+
+    def middle(self, j):
+        if j not in self.middles:
+            a = {}
+            for (c, y, z), f in self.fields(j, "own").items():
+                a[c, 1, y, z] = f[1] - f[0]
+                if y or z:
+                    a[c, 0, y, z] = f[0] + f[1]
+            g = modal(a, self.em_at(j, 1))
+            parts = {}
+            for c, y, z in self.fields(j, "own"):
+                gd = g[c, 1, y, z]
+                if y or z:
+                    gs = g[c, 0, y, z]
+                    parts[c, y, z] = gs - gd, gs + gd
+                else:
+                    parts[c, y, z] = -gd, gd
+            self.middles[j] = parts
+        return self.middles[j]
+
+    def begin(self):
+        for j in range(1, 8):
+            self.middle(j)
+
+    def element(self, j):
+        if j not in self.elements:
+            own, outer, parts = self.fields(j, "own"), self.fields(j, "outer"), self.middle(j)
+            a = {}
+            for c, y, z in own:
+                fo, fh = own[c, y, z], outer[c, y, z]
+                a[c, 1, y, z] = jnp.stack([fo[0] - fh[0], fh[1] - fo[1]])
+                if y or z:
+                    a[c, 0, y, z] = fo + fh
+            g = modal(a, self.em_at(j, 0, 2))
+            h = {}
+            for c, y, z in own:
+                p1, p2 = parts[c, y, z]
+                gd = g[c, 1, y, z]
+                if y or z:
+                    gs = g[c, 0, y, z]
+                    p1, p2 = p1 + gs[0], p2 + gs[1]
+                h[c, y, z] = jnp.stack([p1 + gd[0], p2 - gd[1]])
+            lows = [[h[c, 0, z] - h[c, 1, z] for z in (0, 1)] for c in range(3)]
+            highs = [[h[c, 0, z] + h[c, 1, z] for z in (0, 1)] for c in range(3)]
             self.elements[j] = lows, highs
         return self.elements[j]
 
@@ -480,53 +509,71 @@
     tell_x(0)
     tell_y(0)
     mark('wait1')
+    wait_in(None, 16, rows_of(176))
+    low = sub < 4
+
+    def spread(ref, k, y):
+        return jnp.where(low, ref[0, k, y:y + 1], ref[1, k, y:y + 1])
+
+    def at(y):
+        return pl.ds(8 * y, 8)
+
+    def start_tile(p, comp, r):
+        if r in (0, 9):
+            t = yrow[p + 4 * (r == 9), pl.ds(comp, 8, stride=4), :]
+        else:
+            t = nat[3 * p + comp, pl.ds(r - 1, 8, stride=8), :]
+        u0[comp, p, r] = jnp.where(valid, t, 0.0)
+
+    for j in range(1, 9):
+        for e in (1, 2):
+            em[j, e] = spread(enat, e, j - 1) * (MU / 16.0)
+        mob[:, at(j - 1)] = jnp.stack([spread(enat, 3, j - 1), spread(enat, 4, j - 1)])
+        for p in (1, 2):
+            for comp in range(3):
+                start_tile(p, comp, j)
+
+    def em_at(j, *es):
+        return em[j, es[0]] if len(es) == 1 else jnp.stack([em[j, e] for e in es])
+
+    def planes_of(u):
+        def planes(c, r, which):
+            return u[c, 1:3, r] if which == "own" else jnp.stack([u[c, 0, r], u[c, 3, r]])
+
+        return planes
+
+    stiff = Stiffness(planes_of(u0), em_at, lambda y, force: first(y, force), lane, sub)
+    stiff.begin()
     for (dx, dy), index in slot.items():
         wait_in(exists[-dx, -dy], index, rows_of(bytes1[dx, dy]))
-    wait_in(None, 16, rows_of(176))
     hear_x(0)
     tell_x(1)
     hear_y(0)
     tell_y(1)
     mark('build')
 
-    low = sub < 4
-
-    def spread(ref, k, y):
-        return jnp.where(low, ref[0, k, y:y + 1], ref[1, k, y:y + 1])
-
     for j in range(9):
         for e in range(3):
             if j == 0:
-                t = jnp.where(low, yrow[e, 12:13], yrow[e, 28:29])
-            else:
-                t = spread(enat, e, j - 1)
-            em[j, e] = t * (MU / 16.0)
+                em[j, e] = jnp.where(low, yrow[e, 12:13], yrow[e, 28:29]) * (MU / 16.0)
+            elif e == 0:
+                em[j, e] = spread(enat, e, j - 1) * (MU / 16.0)
     for y in range(8):
         rows = em[y] + em[y + 1]
         around = rows[0:2] + rows[1:3]
         esum = (around + z_dn(around, lane, sub)) * (16.0 / MU)
-        m = jnp.stack([spread(enat, 3, y), spread(enat, 4, y)])
+        m = mob[:, at(y)]
         guarded = jnp.where(m > 0, esum, 1.0)
-        mob[:, 8 * y:8 * y + 8] = m
-        scl[:, 8 * y:8 * y + 8] = m / (K00 * guarded) + (1.0 - m)
-
+        scl[:, at(y)] = m / (K00 * guarded) + (1.0 - m)
     for r in range(10):
         for p in range(4):
-            for comp in range(3):
-                if r == 0:
-                    t = yrow[p, pl.ds(comp, 8, stride=4), :]
-                elif r == 9:
-                    t = yrow[4 + p, pl.ds(comp, 8, stride=4), :]
-                else:
-                    t = nat[3 * p + comp, pl.ds(r - 1, 8, stride=8), :]
-                u0[comp, p, r] = jnp.where(valid, t, 0.0)
+            if r in (0, 9) or p in (0, 3):
+                for comp in range(3):
+                    start_tile(p, comp, r)
 
     mark('waitq')
     wait_in(None, 17, view(qnat, full, other_rows))
     mark('k1')
-
-    def at(y):
-        return pl.ds(8 * y, 8)
 
     def halo_views(u, key, chunk):
         dx, dy = key
@@ -597,10 +644,6 @@
             rb[gz, comp, :, at(y)] = res
             u1[comp, 1:3, 1 + y] = m * (s * res)
 
-    def em_row(j):
-        return em[j]
-
-    stiff = Stiffness(lambda c, r: u0[c, :, r], em_row, first, lane, sub)
     stiff.rows(0, 7, 1, 6)
     for key in exists:
         wait_out(exists[key], slot[key], rows_of(bytes1[key]))
@@ -609,6 +652,8 @@
     stiff.rows(2, 3, 4, 5)
     send_halos(u1, 8, 1)
     share(rb, 8, 18)
+    stiff = Stiffness(planes_of(u1), em_at, lambda y, force: second(y, force), lane, sub)
+    stiff.begin()
     mark('wait2')
     take_halos(u1, 8, 0)
     take_halos(u1, 8, 1)
@@ -623,7 +668,6 @@
             ib[gz, comp, :, at(y)] = image
             u2[comp, 1:3, 1 + y] = m * (s * image)
 
-    stiff = Stiffness(lambda c, r: u1[c, :, r], em_row, second, lane, sub)
     stiff.rows(0, 7)
     stiff.rows(1, 6)
     sent_halos(u1)
@@ -667,6 +711,8 @@
 
     sums = grams(make_g) + grams(make_h) + grams(make_p)
 
+    stiff = Stiffness(planes_of(u2), em_at, lambda y, force: third(y, force), lane, sub)
+    stiff.begin()
     mark('wait3')
     take_halos(u2, 0, 0)
     mark('k3')
@@ -687,7 +733,6 @@
             else:
                 jacc.append(prods)
 
-    stiff = Stiffness(lambda c, r: u2[c, :, r], em_row, third, lane, sub)
     stiff.rows(0, 7)
     take_halos(u2, 0, 1)
     stiff.rows(1, 6, 2, 3, 4, 5)

time: 74.5 us -> 74.1 us (level)
  no operation moved by 1% of the time
where the time goes in v7:
time: 74.1 us; the launch traced here: 73.9 us
  Pallas kernels  71.5 us (96%)
  other arithmetic  1.72 us (2%)
    pallas_call x1, Pallas kernels, shards(): pl.pallas_call(functools.partial(kernel, nx, ny), out_shape=(out, out), i...  71.5 us
    sub x1, other arithmetic, shards(): return (start + change, shifted - start)  1.72 us

profile of v7, /device:TPU:65, one launch (start us, length us, event | category | flops | bytes accessed | tf_op | source)
XLA Modules:
  0.0 73.9 jit_solution(12552680039818913928)
XLA Ops:
  0.6 0.0 copy-start
  0.6 71.5 %shard_map.77 = (f32[6,3,2,8,128]{4,3,2,1,0:T(8,128)}, f32[6,3,2,8,128]{4,3,2,1,0:T(8,128)}) custom-call(s32[6,16]{1,0:T(8,128)} %n_hbm.1, f32[6,3,16]{2,1,0:T(4,128)} %bitcast.1, f32[6,3,2,8,128]{4,3,2,1,0:T(8,128)} %x_hbm.1, f32[6,3,2,8,128]{4,3,2,1,0:T(8,128)} %b_hbm.1, s32[2,8,128]{2,1,0:T(8,128)} %d_hbm.1, s32[2,8,128]{2,1,0:T(8,128)} %s_hbm.1), custom_call_target="tpu_custom_call" | custom-call | tf_op jit(solution)/shard_map/pallas_call | solution.py:896
  72.2 0.0 copy-done
  72.2 1.7 %fusion = (f32[6,3,2,8,128]{4,3,2,1,0:T(8,128)}, f32[6,3,2,8,128]{4,3,2,1,0:T(8,128)}) fusion(f32[6,3,2,8,128]{4,3,2,1,0:T(8,128)} %get-tuple-element.5, f32[6,3,2,8,128]{4,3,2,1,0:T(8,128)S(1)} %copy-done, f32[6,3,2,8,128]{4,3,2,1,0:T(8,128)} %get-tuple-element.4), kind=kLoop, calls=%fused_computation | loop fusion | flops 73728 | bytes 737280 | tf_op jit(solution)/shard_map/sub | solution.py:905
Async XLA Ops:
  0.6 71.5 %copy-start = (f32[6,3,2,8,128]{4,3,2,1,0:T(8,128)S(1)}, f32[6,3,2,8,128]{4,3,2,1,0:T(8,128)}, u32[]{:S(2)}) copy-start(f32[6,3,2,8,128]{4,3,2,1,0:T(8,128)} %x_hbm.1) | copy-start | bytes 442372

commit v8 on v7

--- a/solution.py
+++ b/solution.py
@@ -218,7 +218,7 @@
     xo_hbm, ro_hbm,
     xin, bin_, din, sin, xm, ysend, esend, qs,
     nat, yrow, enat, qnat,
-    u0, u1, u2, em, mob, scl, rb, ib, yb, ga, ag, bg, dummy, xout, rout, nodes, vals,
+    u0, u1, u2, em, mob, scl, rb, ib, yb, ga, ag, bg, ag2, bg2, vout, wout, dummy, xout, rout, nodes, vals,
     in_sem, out_sem, ss, rs, heard,
 ):
     grp, gx, gy, gz = (lax.axis_index(a) for a in ("grp", "gx", "gy", "gz"))
@@ -582,7 +582,7 @@
         if dy == 0:
             return [
                 (view(u, full, src, pl.ds(k, m)), view(u, full, dst, pl.ds(k, m)))
-                for k, m in (((1, 2), (7, 1)) if chunk == 0 else ((3, 3),))
+                for k, m in ((1 + 3 * chunk, 3),)
             ]
         if dx == 0:
             return [(view(u, full, pl.ds(1, 2), ysrc), view(u, full, pl.ds(1, 2), ydst))]
@@ -591,7 +591,7 @@
     halo_rows = {(dx, dy): 8 * 3 * (6 if dy == 0 else 2 if dx == 0 else 1) for dx, dy in exists}
 
     free = sub % 4 == 3
-    chunks = ((1, 2, 7, 8), (3, 4, 5, 6))
+    chunks = ((1, 2, 3, 8), (4, 5, 6, 7))
 
     def pack(u, chunk):
         *carriers, last = chunks[chunk]
@@ -644,16 +644,20 @@
             rb[gz, comp, :, at(y)] = res
             u1[comp, 1:3, 1 + y] = m * (s * res)
 
-    stiff.rows(0, 7, 1, 6)
+    stiff.rows(0, 7, 1, 2)
     for key in exists:
         wait_out(exists[key], slot[key], rows_of(bytes1[key]))
     wait_out(None, 8, rows_of(176))
     send_halos(u1, 8, 0)
-    stiff.rows(2, 3, 4, 5)
+    stiff.rows(3, 4, 5, 6)
     send_halos(u1, 8, 1)
     share(rb, 8, 18)
     stiff = Stiffness(planes_of(u1), em_at, lambda y, force: second(y, force), lane, sub)
     stiff.begin()
+    hear_x(1)
+    tell_x(2)
+    hear_y(1)
+    tell_y(2)
     mark('wait2')
     take_halos(u1, 8, 0)
     take_halos(u1, 8, 1)
@@ -668,19 +672,14 @@
             ib[gz, comp, :, at(y)] = image
             u2[comp, 1:3, 1 + y] = m * (s * image)
 
-    stiff.rows(0, 7)
-    stiff.rows(1, 6)
+    stiff.rows(0, 7, 1, 2)
     sent_halos(u1)
     send_halos(u2, 0, 0)
-    stiff.rows(2, 3, 4, 5)
+    stiff.rows(3, 4, 5, 6)
     send_halos(u2, 0, 1)
     mark('send3')
     wait_out(None, 9, view(qs, oz))
     share(ib, 9, 19)
-    hear_x(1)
-    tell_x(2)
-    hear_y(1)
-    tell_y(2)
     wait_in(None, 18, view(rb, oz))
     wait_in(None, 19, view(ib, oz))
 
@@ -709,7 +708,52 @@
         r, ro = own_other(rb, comp, y)
         return r, ro, s * r
 
-    sums = grams(make_g) + grams(make_h) + grams(make_p)
+    me = gz * ny + gy
+
+    def send_row(accs, rows_ref, send_index, recv_index):
+        folded = [a + pltpu.roll(a, 4, axis=0) for a in accs]
+        if len(folded) % 2:
+            folded.append(folded[-1])
+        for t in range(len(folded) // 2):
+            ga[pl.ds(8 * t, 8), :] = jnp.where(low, folded[2 * t], folded[2 * t + 1])
+        row = lax.dot_general(
+            jnp.ones((8, 128), f32), ga[...], (((1,), (1,)), ((), ())),
+            precision=lax.Precision.HIGHEST, preferred_element_type=f32,
+        )
+        rows_ref[me] = row[0:1]
+        exchange(None, send_index, recv_index, [
+            (view(rows_ref, me), view(rows_ref, me), (grp, gx, lax.rem(gy + d, ny), oz if flip else gz))
+            for d in sorted(range(ny), key=lambda d: -min(d, ny - d)) for flip in (0, 1) if d or flip
+        ])
+
+    def sum_rows(rows_ref, recv_index, planes_ref):
+        wait_in(None, recv_index, view(rows_ref, pl.ds(0, 2 * ny - 1)))
+        for s in (0, 1):
+            total = rows_ref[s * ny]
+            for k in range(1, ny):
+                total = total + rows_ref[s * ny + k]
+            planes_ref[gx, s:s + 1] = total
+
+    def send_planes(planes_ref, send_index, recv_index, first_plane, last_plane):
+        def send_sum(target, carry):
+            mine = view(planes_ref, gx)
+            descriptor(mine, mine, send_index, recv_index, (grp, target, gy, gz)).start()
+            return carry
+
+        lax.fori_loop(first_plane, last_plane, send_sum, 0)
+
+    def totals(planes_ref, recv_index):
+        wait_in(None, recv_index, view(planes_ref, pl.ds(0, nx - 1)))
+        total = planes_ref[0]
+        for k in range(1, nx):
+            total = total + planes_ref[k]
+        return [jnp.broadcast_to(total[s:s + 1], (8, 128)) for s in (0, 1)]
+
+    ga[...] = jnp.zeros_like(ga)
+    hear_x(2)
+    tell_x(3)
+    hear_y(2)
+    send_row(grams(make_g) + grams(make_h) + grams(make_p), ag2, 12, 27)
 
     stiff = Stiffness(planes_of(u2), em_at, lambda y, force: third(y, force), lane, sub)
     stiff.begin()
@@ -733,56 +777,25 @@
             else:
                 jacc.append(prods)
 
-    stiff.rows(0, 7)
+    stiff.rows(0, 1)
     take_halos(u2, 0, 1)
-    stiff.rows(1, 6, 2, 3, 4, 5)
+    stiff.rows(7, 2, 3, 4, 5, 6)
     wait_out(None, 8, view(rb, gz))
     share(yb, 8, 20)
-    sums = sums + [a[0] + a[1] for a in jacc[0]]
-
     mark('rowsum')
-    folded = [a + pltpu.roll(a, 4, axis=0) for a in sums]
-    ga[pl.ds(80, 48), :] = jnp.zeros((48, 128), f32)
-    for t in range(10):
-        ga[pl.ds(8 * t, 8), :] = jnp.where(low, folded[2 * t], folded[2 * t + 1])
-    row = lax.dot_general(
-        jnp.ones((8, 128), f32), ga[...], (((1,), (1,)), ((), ())),
-        precision=lax.Precision.HIGHEST, preferred_element_type=f32,
-    )
-    hear_y(2)
+    send_row([a[0] + a[1] for a in jacc[0]], ag, 10, 21)
     mark('reduce_a')
-    me = gz * ny + gy
-    ag[me] = row[0:1]
-    exchange(None, 10, 21, [
-        (view(ag, me), view(ag, me), (grp, gx, lax.rem(gy + d, ny), oz if flip else gz))
-        for d in sorted(range(ny), key=lambda d: -min(d, ny - d)) for flip in (0, 1) if d or flip
-    ])
-    hear_x(2)
-    tell_x(3)
-    wait_in(None, 21, view(ag, pl.ds(0, 2 * ny - 1)))
-    for s in (0, 1):
-        total = ag[s * ny]
-        for k in range(1, ny):
-            total = total + ag[s * ny + k]
-        bg[gx, s:s + 1] = total
+    sum_rows(ag2, 27, bg2)
     hear_x(3, above=False)
+    send_planes(bg2, 13, 28, 0, gx)
+    sum_rows(ag, 21, bg)
     mark('reduce_b')
-    def send_sum(target, carry):
-        descriptor(view(bg, gx), view(bg, gx), 11, 22, (grp, target, gy, gz)).start()
-        return carry
-
-    lax.fori_loop(0, gx, send_sum, 0)
+    send_planes(bg, 11, 22, 0, gx)
     hear_x(3, below=False)
-    lax.fori_loop(gx + 1, nx, send_sum, 0)
-    wait_in(None, 22, view(bg, pl.ds(0, nx - 1)))
-    mark('solve')
-    total = bg[0]
-    for k in range(1, nx):
-        total = total + bg[k]
-
-    rows = [jnp.broadcast_to(total[s:s + 1], (8, 128)) for s in (0, 1)]
-
-    def entry(matrix, i, j):
+    send_planes(bg, 11, 22, gx + 1, nx)
+    send_planes(bg2, 13, 28, gx + 1, nx)
+
+    def entry(rows, matrix, i, j):
         ci, ki = divmod(i, HALF)
         cj, kj = divmod(j, HALF)
         if ci == cj:
@@ -801,22 +814,22 @@
         return jnp.broadcast_to(rows[s][:, where:where + 1], (8, 128))
 
     n = CASES
-    mats = []
-    for matrix in range(4):
+
+    def matrix_of(rows, matrix):
         m = {}
         for i in range(n):
             for j in range(i + 1):
-                m[i, j] = entry(matrix, i, j)
-                m[j, i] = m[i, j]
-        mats.append(m)
-    mg, mh, mp, mj = mats
-
+                m[i, j] = m[j, i] = entry(rows, matrix, i, j)
+        return m
+
+    rows = totals(bg2, 28)
+    mg, mh, mp = (matrix_of(rows, matrix) for matrix in range(3))
     lo1, inv1 = cholesky(mg, n)
     zh = [forward(lo1, inv1, [mh[i, j] for i in range(n)], n) for j in range(n)]
     zp = [forward(lo1, inv1, [mp[i, j] for i in range(n)], n) for j in range(n)]
     th = [backward(lo1, inv1, zh[j], n) for j in range(n)]
     al = [backward(lo1, inv1, zp[j], n) for j in range(n)]
-    schur, right = {}, []
+    right = []
     for j in range(n):
         col = []
         for i in range(n):
@@ -824,25 +837,15 @@
             for k in range(n):
                 t = t - zh[i][k] * zp[j][k]
             col.append(t)
-            if i >= j:
-                t = mj[i, j]
-                for k in range(n):
-                    t = t - zh[i][k] * zh[j][k]
-                schur[i, j] = t
         right.append(col)
-    lo2, inv2 = cholesky(schur, n)
-    cb = [backward(lo2, inv2, forward(lo2, inv2, right[j], n), n) for j in range(n)]
-    ca = []
+    taken = {}
     for j in range(n):
-        col = []
-        for i in range(n):
-            t = al[j][i]
-            for k in range(n):
-                t = t - th[k][i] * cb[j][k]
-            col.append(t)
-        ca.append(col)
-
-    mark('combine')
+        for i in range(j, n):
+            t = zh[i][0] * zh[j][0]
+            for k in range(1, n):
+                t = t + zh[i][k] * zh[j][k]
+            taken[i, j] = t
+
     wait_in(None, 20, view(yb, oz))
     for comp in range(3):
         for p in range(2):
@@ -855,13 +858,36 @@
                 fi.append(ib[core, comp, p, pick, :])
                 fy.append(yb[core, comp, p, pick, :])
             for i in range(n):
-                up = fr[0] * ca[i][0] + fi[0] * cb[i][0]
-                dn = fi[0] * ca[i][0] + fy[0] * cb[i][0]
+                up, dn, v, y = fr[0] * al[i][0], fi[0] * al[i][0], fr[0] * th[i][0], fi[0] * th[i][0]
                 for j in range(1, n):
-                    up = up + fr[j] * ca[i][j] + fi[j] * cb[i][j]
-                    dn = dn + fi[j] * ca[i][j] + fy[j] * cb[i][j]
+                    up = up + fr[j] * al[i][j]
+                    dn = dn + fi[j] * al[i][j]
+                    v = v + fr[j] * th[i][j]
+                    y = y + fi[j] * th[i][j]
                 xout[i, comp, p] = s * up
                 rout[i, comp, p] = (fr[i] - dn) + xin[i, comp, p]
+                vout[i, comp, p] = s * (fi[i] - v)
+                wout[i, comp, p] = fy[i] - y
+
+    mark('solve')
+    rows = totals(bg, 22)
+    mj = matrix_of(rows, 0)
+    schur = {key: mj[key] - t for key, t in taken.items()}
+    lo2, inv2 = cholesky(schur, n)
+    cb = [backward(lo2, inv2, forward(lo2, inv2, right[j], n), n) for j in range(n)]
+
+    mark('combine')
+    for comp in range(3):
+        for p in range(2):
+            v = [vout[j, comp, p] for j in range(n)]
+            w = [wout[j, comp, p] for j in range(n)]
+            for i in range(n):
+                up, dn = v[0] * cb[i][0], w[0] * cb[i][0]
+                for j in range(1, n):
+                    up = up + v[j] * cb[i][j]
+                    dn = dn + w[j] * cb[i][j]
+                xout[i, comp, p] = xout[i, comp, p] + up
+                rout[i, comp, p] = rout[i, comp, p] - dn
         for i, (src, dst) in enumerate(((xout, xo_hbm), (rout, ro_hbm))):
             pltpu.make_async_copy(src.at[:, comp], dst.at[:, comp], out_sem.at[i]).start()
     mark('drain')
@@ -870,6 +896,8 @@
     wait_out(None, 9, view(ib, gz))
     wait_out(None, 10, view(ag, pl.ds(0, 2 * ny - 1)))
     wait_out(None, 11, view(bg, pl.ds(0, nx - 1)))
+    wait_out(None, 12, view(ag2, pl.ds(0, 2 * ny - 1)))
+    wait_out(None, 13, view(bg2, pl.ds(0, nx - 1)))
     for i, (src, dst) in enumerate(((xout, xo_hbm), (rout, ro_hbm))):
         pltpu.make_async_copy(src, dst, out_sem.at[i]).wait()
     mark(None)
@@ -887,9 +915,10 @@
         vmem(3, 4, 10, 8, 128), vmem(3, 4, 10, 8, 128), vmem(3, 4, 10, 8, 128),
         vmem(9, 3, 8, 128), vmem(2, 64, 128), vmem(2, 64, 128),
         vmem(2, 3, 2, 64, 128), vmem(2, 3, 2, 64, 128), vmem(2, 3, 2, 64, 128),
-        vmem(128, 128), vmem(2 * ny, 1, 128), vmem(nx, 2, 128), vmem(176, 128), vmem(*block), vmem(*block),
+        vmem(128, 128), vmem(2 * ny, 1, 128), vmem(nx, 2, 128),
+        vmem(2 * ny, 1, 128), vmem(nx, 2, 128), vmem(*block), vmem(*block), vmem(176, 128), vmem(*block), vmem(*block),
         pltpu.SMEM(load_nodes.shape, jnp.int32), pltpu.SMEM((CASES, 3, LOADS), f32),
-        pltpu.SemaphoreType.DMA((6,)), pltpu.SemaphoreType.DMA((2,)), pltpu.SemaphoreType.DMA((12,)), pltpu.SemaphoreType.DMA((27,)),
+        pltpu.SemaphoreType.DMA((6,)), pltpu.SemaphoreType.DMA((2,)), pltpu.SemaphoreType.DMA((14,)), pltpu.SemaphoreType.DMA((29,)),
         pltpu.SemaphoreType.REGULAR((14,)),
     ]
     out = jax.ShapeDtypeStruct(block, f32)

time: 74.1 us -> 73.8 us (level)
  no operation moved by 1% of the time
where the time goes in v8:
time: 73.8 us; the launch traced here: 73.6 us
  Pallas kernels  71.2 us (96%)
  other arithmetic  1.72 us (2%)
    pallas_call x1, Pallas kernels, shards(): pl.pallas_call(functools.partial(kernel, nx, ny), out_shape=(out, out), i...  71.2 us
    sub x1, other arithmetic, shards(): return (start + change, shifted - start)  1.72 us

profile of v8, /device:TPU:65, one launch (start us, length us, event | category | flops | bytes accessed | tf_op | source)
XLA Modules:
  0.0 73.6 jit_solution(8805786494776114983)
XLA Ops:
  0.6 0.0 copy-start
  0.6 71.2 %shard_map.77 = (f32[6,3,2,8,128]{4,3,2,1,0:T(8,128)}, f32[6,3,2,8,128]{4,3,2,1,0:T(8,128)}) custom-call(s32[6,16]{1,0:T(8,128)} %n_hbm.1, f32[6,3,16]{2,1,0:T(4,128)} %bitcast.1, f32[6,3,2,8,128]{4,3,2,1,0:T(8,128)} %x_hbm.1, f32[6,3,2,8,128]{4,3,2,1,0:T(8,128)} %b_hbm.1, s32[2,8,128]{2,1,0:T(8,128)} %d_hbm.1, s32[2,8,128]{2,1,0:T(8,128)} %s_hbm.1), custom_call_target="tpu_custom_call" | custom-call | tf_op jit(solution)/shard_map/pallas_call | solution.py:925
  71.9 0.0 copy-done
  71.9 1.7 %fusion = (f32[6,3,2,8,128]{4,3,2,1,0:T(8,128)}, f32[6,3,2,8,128]{4,3,2,1,0:T(8,128)}) fusion(f32[6,3,2,8,128]{4,3,2,1,0:T(8,128)} %get-tuple-element.5, f32[6,3,2,8,128]{4,3,2,1,0:T(8,128)S(1)} %copy-done, f32[6,3,2,8,128]{4,3,2,1,0:T(8,128)} %get-tuple-element.4), kind=kLoop, calls=%fused_computation | loop fusion | flops 73728 | bytes 737280 | tf_op jit(solution)/shard_map/sub | solution.py:934
Async XLA Ops:
  0.6 71.2 %copy-start = (f32[6,3,2,8,128]{4,3,2,1,0:T(8,128)S(1)}, f32[6,3,2,8,128]{4,3,2,1,0:T(8,128)}, u32[]{:S(2)}) copy-start(f32[6,3,2,8,128]{4,3,2,1,0:T(8,128)} %x_hbm.1) | copy-start | bytes 442372

commit v9 on v8

--- a/solution.py
+++ b/solution.py
@@ -750,13 +750,14 @@
         return [jnp.broadcast_to(total[s:s + 1], (8, 128)) for s in (0, 1)]
 
     ga[...] = jnp.zeros_like(ga)
+    early = grams(make_g) + grams(make_h) + grams(make_p)
+
+    stiff = Stiffness(planes_of(u2), em_at, lambda y, force: third(y, force), lane, sub)
+    stiff.begin()
     hear_x(2)
     tell_x(3)
     hear_y(2)
-    send_row(grams(make_g) + grams(make_h) + grams(make_p), ag2, 12, 27)
-
-    stiff = Stiffness(planes_of(u2), em_at, lambda y, force: third(y, force), lane, sub)
-    stiff.begin()
+    send_row(early, ag2, 12, 27)
     mark('wait3')
     take_halos(u2, 0, 0)
     mark('k3')

time: 73.8 us -> 73.8 us (level)
  no operation moved by 1% of the time
where the time goes in v9:
time: 73.8 us; the launch traced here: 73.6 us
  Pallas kernels  71.2 us (96%)
  other arithmetic  1.72 us (2%)
    pallas_call x1, Pallas kernels, shards(): pl.pallas_call(functools.partial(kernel, nx, ny), out_shape=(out, out), i...  71.2 us
    sub x1, other arithmetic, shards(): return (start + change, shifted - start)  1.72 us

profile of v9, /device:TPU:65, one launch (start us, length us, event | category | flops | bytes accessed | tf_op | source)
XLA Modules:
  0.0 73.6 jit_solution(11075601788400623720)
XLA Ops:
  0.6 0.0 copy-start
  0.6 71.2 %shard_map.77 = (f32[6,3,2,8,128]{4,3,2,1,0:T(8,128)}, f32[6,3,2,8,128]{4,3,2,1,0:T(8,128)}) custom-call(s32[6,16]{1,0:T(8,128)} %n_hbm.1, f32[6,3,16]{2,1,0:T(4,128)} %bitcast.1, f32[6,3,2,8,128]{4,3,2,1,0:T(8,128)} %x_hbm.1, f32[6,3,2,8,128]{4,3,2,1,0:T(8,128)} %b_hbm.1, s32[2,8,128]{2,1,0:T(8,128)} %d_hbm.1, s32[2,8,128]{2,1,0:T(8,128)} %s_hbm.1), custom_call_target="tpu_custom_call" | custom-call | tf_op jit(solution)/shard_map/pallas_call | solution.py:926
  71.9 0.0 copy-done
  71.9 1.7 %fusion = (f32[6,3,2,8,128]{4,3,2,1,0:T(8,128)}, f32[6,3,2,8,128]{4,3,2,1,0:T(8,128)}) fusion(f32[6,3,2,8,128]{4,3,2,1,0:T(8,128)} %get-tuple-element.5, f32[6,3,2,8,128]{4,3,2,1,0:T(8,128)S(1)} %copy-done, f32[6,3,2,8,128]{4,3,2,1,0:T(8,128)} %get-tuple-element.4), kind=kLoop, calls=%fused_computation | loop fusion | flops 73728 | bytes 737280 | tf_op jit(solution)/shard_map/sub | solution.py:935
Async XLA Ops:
  0.6 71.2 %copy-start = (f32[6,3,2,8,128]{4,3,2,1,0:T(8,128)S(1)}, f32[6,3,2,8,128]{4,3,2,1,0:T(8,128)}, u32[]{:S(2)}) copy-start(f32[6,3,2,8,128]{4,3,2,1,0:T(8,128)} %x_hbm.1) | copy-start | bytes 442372
